TPU v7x, 32 devices: a whole 2x2x4 slice. The times are simulated.
32 devices in a mesh: tm: 2 (over x), py: 4 (over y, core), pz: 4 (over z).
Axes of the slice: x: 2, y: 2, z: 4, core: 2. Of those that a mesh axis runs over, the one named last changes fastest.
Arguments:
- start_states: float32 [2, 3, 128, 8, 16, 128], P('tm', None, None, None, ('py', 'pz')), may hold values from -6 to 6
Outputs:
- new_states: float32 [2, 3, 128, 8, 16, 128], P('tm', None, None, None, ('py', 'pz'))
All inputs are finite; a program needn't handle non-finite values.
Results may differ from a plain program's by a relative error of at most 0.0001.
Values sent between devices are 32-bit elements; how exact they have to be, the bound alone decides.
A program may use at most 128 MiB of HBM per device.

v0:
```python
from functools import partial
import math

import jax
import jax.numpy as jnp
from jax import lax
import numpy as np
from jax.experimental import pallas as pl
from jax.experimental.pallas import tpu as pltpu
from jax.sharding import PartitionSpec as P

M = 64


viscosity = 0.03
time_step = 0.004
highest = lax.Precision.HIGHEST


def shifted(block, axis, distance):
    devices = range(lax.axis_size(axis))
    route = [(i - distance, i) for i in devices if i - distance in devices]
    return lax.ppermute(block, axis, route)


def signed_wave(places, length):
    return jnp.where(places < length // 2, places, places - length)


def rotate(values):
    halfway = values.shape[-1] // 2
    return jnp.concatenate([-values[..., halfway:], values[..., :halfway]], axis=-1)


def trig_pair(outer, inner, extent, factor):
    residue = jnp.mod(outer[:, None] * inner[None, :], extent)
    radians = residue.astype(jnp.float32) * (2.0 * math.pi / extent)
    return (jnp.cos(radians) * factor, jnp.sin(radians) * factor)


def complex_apply(cosine_part, sine_part, values, contracted, direction_sign):
    kernel = jnp.stack(
        [
            jnp.stack([cosine_part, -direction_sign * sine_part]),
            jnp.stack([direction_sign * sine_part, cosine_part]),
        ]
    )
    halfway = values.shape[-1] // 2
    split = values.reshape(values.shape[:-1] + (2, halfway))
    if contracted == 1:
        pattern = "pqok,fkaqh->foaph"
    else:
        pattern = "pqok,flkqh->floph"
    result = jnp.einsum(pattern, kernel, split, precision=highest)
    return result.reshape(result.shape[:-2] + (2 * halfway,))


def inverse_z(extent, retained):
    halfway = retained // 2
    columns = jnp.arange(retained, dtype=jnp.int32)
    harmonic = columns % halfway
    weight = jnp.where(harmonic == 0, 1.0, 2.0) * retained ** (-0.5)
    residue = jnp.mod(harmonic[:, None] * jnp.arange(extent, dtype=jnp.int32)[None, :], extent)
    radians = residue.astype(jnp.float32) * (2.0 * math.pi / extent)
    return (
        jnp.where((columns < halfway)[:, None], jnp.cos(radians), -jnp.sin(radians))
        * weight[:, None]
    )


def forward_z(extent, retained):
    halfway = retained // 2
    columns = jnp.arange(retained, dtype=jnp.int32)
    harmonic = columns % halfway
    residue = jnp.mod(jnp.arange(extent, dtype=jnp.int32)[:, None] * harmonic[None, :], extent)
    radians = residue.astype(jnp.float32) * (2.0 * math.pi / extent)
    return jnp.where((columns < halfway)[None, :], jnp.cos(radians), -jnp.sin(radians)) * (
        math.sqrt(retained) / extent
    )


def inverse_tail(portion, extent, sectioned, layout):
    count_py, count_pz, groups, member = layout
    retained = portion.shape[2]
    local_rows = retained // groups
    places = jnp.arange(retained, dtype=jnp.int32)
    owners = places // local_rows
    wave_y = signed_wave(places % local_rows * groups + owners, retained)
    points = jnp.arange(extent, dtype=jnp.int32)
    cosine_part, sine_part = trig_pair(points, wave_y, extent, retained ** (-0.5))
    along_y = complex_apply(cosine_part, sine_part, portion, 2, 1.0)
    return jnp.einsum("flyr,rz->flyz", along_y, inverse_z(extent, retained), precision=highest)


def forward_tail(portion, retained, sectioned, layout):
    count_py, count_pz, groups, member = layout
    extent = portion.shape[1]
    local_rows = extent // groups
    places = jnp.arange(extent, dtype=jnp.int32)
    points = places // local_rows * local_rows + places % local_rows
    wave_x = signed_wave(jnp.arange(retained, dtype=jnp.int32), retained)
    cosine_part, sine_part = trig_pair(wave_x, points, extent, math.sqrt(retained) / extent)
    return complex_apply(cosine_part, sine_part, portion, 1, -1.0)


def to_physical(coeffs, wavegrid, extent, resolution, layout):
    wave_x, wave_y, wave_z = wavegrid
    retained = coeffs.shape[1]
    seeds = jnp.concatenate([coeffs, wave_x * coeffs[1:3]], axis=0)
    points = jnp.arange(extent, dtype=jnp.int32)
    wave_rows = signed_wave(jnp.arange(retained, dtype=jnp.int32), retained)
    cosine_part, sine_part = trig_pair(points, wave_rows, extent, retained ** (-0.5))
    moved_x = complex_apply(cosine_part, sine_part, seeds, 1, 1.0)
    curl_x = rotate(wave_y * moved_x[2] - wave_z * moved_x[1])
    curl_y = rotate(wave_z * moved_x[0] - moved_x[4])
    curl_z = rotate(moved_x[3] - wave_y * moved_x[0])
    spread = jnp.concatenate([moved_x[:3], jnp.stack([curl_x, curl_y, curl_z])], axis=0)
    if resolution == "coarse":
        finish = partial(inverse_tail, extent=extent, sectioned=False, layout=layout)
        return finish(lax.all_to_all(spread, ("py", "pz"), split_axis=1, concat_axis=2, tiled=True))
    else:
        finish = partial(inverse_tail, extent=extent, sectioned=False, layout=layout)
        return finish(lax.all_to_all(spread, ("py", "pz"), split_axis=1, concat_axis=2, tiled=True))


def to_spectral(fields, retained, resolution, layout):
    count_py, count_pz, groups, member = layout
    extent = fields.shape[-1]
    along_z = jnp.einsum("flyz,zr->flyr", fields, forward_z(extent, retained), precision=highest)
    local_rows = retained // groups
    places = jnp.arange(retained, dtype=jnp.int32)
    wave_y = signed_wave(places % local_rows * groups + places // local_rows, retained)
    cosine_part, sine_part = trig_pair(
        wave_y, jnp.arange(extent, dtype=jnp.int32), extent, math.sqrt(retained) / extent
    )
    along_y = complex_apply(cosine_part, sine_part, along_z, 2, -1.0)
    if resolution == "coarse":
        finish = partial(forward_tail, retained=retained, sectioned=False, layout=layout)
        return finish(
            lax.all_to_all(along_y, ("py", "pz"), split_axis=2, concat_axis=1, tiled=True)
        )
    else:
        finish = partial(forward_tail, retained=retained, sectioned=False, layout=layout)
        return finish(
            lax.all_to_all(along_y, ("py", "pz"), split_axis=2, concat_axis=1, tiled=True)
        )


def wave_grid(retained, layout):
    count_py, count_pz, groups, member = layout
    places = jnp.arange(retained, dtype=jnp.int32)
    wave_x = signed_wave(places, retained).astype(jnp.float32)[:, None, None]
    local_places = jnp.arange(retained // groups, dtype=jnp.int32)
    wave_y = signed_wave(local_places * groups + member, retained).astype(jnp.float32)[
        None, :, None
    ]
    wave_z = (places % (retained // 2)).astype(jnp.float32)[None, None, :]
    return (wave_x, wave_y, wave_z)


def project(coeffs, wavegrid):
    wave_x, wave_y, wave_z = wavegrid
    squared = wave_x * wave_x + wave_y * wave_y + wave_z * wave_z
    divergence = (wave_x * coeffs[0] + wave_y * coeffs[1] + wave_z * coeffs[2]) / jnp.maximum(
        squared, 1.0
    )
    return jnp.stack(
        [
            coeffs[0] - wave_x * divergence,
            coeffs[1] - wave_y * divergence,
            coeffs[2] - wave_z * divergence,
        ]
    )


def cross_product(first_field, second_field):
    return jnp.stack(
        [
            first_field[1] * second_field[2] - first_field[2] * second_field[1],
            first_field[2] * second_field[0] - first_field[0] * second_field[2],
            first_field[0] * second_field[1] - first_field[1] * second_field[0],
        ]
    )


def advance(coeffs, resolution, layout):
    retained = coeffs.shape[1]
    extent = 3 * retained // 2
    wavegrid = wave_grid(retained, layout)
    fields = to_physical(coeffs, wavegrid, extent, resolution, layout)
    product = cross_product(fields[:3], fields[3:])
    nonlinear = to_spectral(product, retained, resolution, layout)
    wave_x, wave_y, wave_z = wavegrid
    squared = wave_x * wave_x + wave_y * wave_y + wave_z * wave_z
    damping = jnp.exp(-viscosity * time_step * squared)
    return damping * (coeffs + time_step * project(nonlinear, wavegrid))


def restrict(coeffs, kept, groups):
    halfway = kept // 2
    retained = coeffs.shape[1]
    rows_kept = jnp.concatenate([coeffs[:, :halfway], coeffs[:, retained - halfway :]], axis=1)
    local_rows = coeffs.shape[2]
    local_kept = kept // groups // 2
    rows_kept = jnp.concatenate(
        [rows_kept[:, :, :local_kept], rows_kept[:, :, local_rows - local_kept :]], axis=2
    )
    columns_half = coeffs.shape[3] // 2
    return jnp.concatenate(
        [rows_kept[..., :halfway], rows_kept[..., columns_half : columns_half + halfway]], axis=3
    )


def prolong(coeffs, retained, groups):
    components, kept, local_kept, width = coeffs.shape
    halfway = kept // 2
    zeros_x = jnp.zeros((components, retained - kept, local_kept, width), jnp.float32)
    wider = jnp.concatenate([coeffs[:, :halfway], zeros_x, coeffs[:, halfway:]], axis=1)
    local_rows = retained // groups
    split_rows = local_kept // 2
    zeros_y = jnp.zeros((components, retained, local_rows - local_kept, width), jnp.float32)
    wider = jnp.concatenate([wider[:, :, :split_rows], zeros_y, wider[:, :, split_rows:]], axis=2)
    zeros_z = jnp.zeros((components, retained, local_rows, retained // 2 - halfway), jnp.float32)
    return jnp.concatenate([wider[..., :halfway], zeros_z, wider[..., halfway:], zeros_z], axis=3)


def wave_table(length):
    places = np.arange(length)
    return np.where(places < length // 2, places, places - length)


def trig_table(outer, inner, extent):
    radians = 2.0 * np.pi / extent * np.mod(np.outer(outer, inner), extent)
    return np.cos(radians), np.sin(radians)


def split_table(table):
    table = np.asarray(table, np.float32)
    high = table.astype(jnp.bfloat16)
    low = (table - high.astype(np.float32)).astype(jnp.bfloat16)
    return high, low


def split(values):
    high = values.astype(jnp.bfloat16)
    low = (values - high.astype(jnp.float32)).astype(jnp.bfloat16)
    return high, low


def dot3(left, right):
    def dot(a, b):
        return jnp.dot(a, b, preferred_element_type=jnp.float32)

    return dot(left[0], right[0]) + dot(left[0], right[1]) + dot(left[1], right[0])


def z_tables(extent, retained):
    halfway = retained // 2
    columns = np.arange(retained)
    harmonic = columns % halfway
    cosine, sine = trig_table(harmonic, np.arange(extent), extent)
    table = np.where((columns < halfway)[:, None], cosine, -sine)
    weight = np.where(harmonic == 0, 1.0, 2.0)[:, None] * retained ** (-0.5)
    return table * weight, table.T * (math.sqrt(retained) / extent)


def plane_tables(extent, retained, groups):
    rows = retained // groups
    places = np.arange(retained)
    wave_y = wave_table(retained)[places % rows * groups + places // rows]
    cosine, sine = trig_table(np.arange(extent), wave_y, extent)
    inverse_y = np.concatenate([cosine, sine], axis=1) * retained ** (-0.5)
    forward_y = np.concatenate([cosine.T, -sine.T], axis=1) * (math.sqrt(retained) / extent)
    inverse_last, forward_last = z_tables(extent, retained)
    halfway = retained // 2
    turn = np.where(places < halfway, -1.0, 1.0)
    wave_z = (places % halfway).astype(np.float32)
    lanes = np.zeros((8, retained), np.float32)
    lanes[0], lanes[1] = turn, wave_z
    column = np.broadcast_to(wave_y[:, None], (retained, retained)).astype(np.float32)
    tables = [lanes, column]
    for table in (inverse_y, inverse_last, forward_last, forward_y):
        tables += split_table(table)
    return [jnp.asarray(t) for t in tables]


def plane_math(fields, tables):
    lanes, wave_y, iy0, iy1, iz0, iz1, fz0, fz1, fy0, fy1 = tables
    turn, wave_z = lanes[0:1, :], lanes[1:2, :]
    retained = wave_y.shape[0]
    extent = iy0.shape[0]

    def turned(values):
        return pltpu.roll(values, retained // 2, 1) * turn

    v0, v1, v2, d1, d2 = fields
    i0 = turned(v0)
    w0 = turned(wave_y * v2 - wave_z * v1)
    w1 = wave_z * i0 - d2
    w2 = d1 - wave_y * i0
    six = (v0, v1, v2, w0, w1, w2)
    stacked = jnp.concatenate(
        [jnp.concatenate(six, axis=1), jnp.concatenate([i0] + [turned(f) for f in six[1:]], axis=1)],
        axis=0,
    )
    along_y = dot3((iy0, iy1), split(stacked))
    rows = jnp.concatenate(
        [along_y[:, f * retained : (f + 1) * retained] for f in range(6)], axis=0
    )
    physical = dot3(split(rows), (iz0, iz1))
    u0, u1, u2, w0, w1, w2 = [physical[f * extent : (f + 1) * extent] for f in range(6)]
    product = jnp.concatenate([u1 * w2 - u2 * w1, u2 * w0 - u0 * w2, u0 * w1 - u1 * w0], axis=0)
    along_z = dot3(split(product), (fz0, fz1))
    parts = [along_z[f * extent : (f + 1) * extent] for f in range(3)]
    stacked = jnp.concatenate(
        [jnp.concatenate(parts, axis=1), jnp.concatenate([turned(p) for p in parts], axis=1)],
        axis=0,
    )
    result = dot3((fy0, fy1), split(stacked))
    return [result[:, f * retained : (f + 1) * retained] for f in range(3)]


def x_tables(extent, retained, halves):
    wave_x = wave_table(retained)
    cosine, sine = trig_table(np.arange(extent), wave_x, extent)
    values = np.concatenate([cosine, sine], axis=1)
    slopes = np.concatenate([-sine * wave_x, cosine * wave_x], axis=1)
    per_half = [table.reshape(halves, extent // halves, -1) for table in (values, slopes)]
    table = np.concatenate(per_half, axis=1) * retained ** (-0.5)
    return [jnp.asarray(t) for t in split_table(table)]


def step_kernel(*refs):
    state, x0, x1 = refs[:3]
    table_refs = refs[3:13]
    out, earlier = refs[13:15]
    spread, recv, result = refs[15:18]
    state_send, state_recv, field_send, field_recv, back_send, back_recv = refs[18:]
    _, planes, groups, rows, retained = spread.shape
    count_pz = lax.axis_size("pz")
    position = lax.axis_index("tm")
    row, place = lax.axis_index("py"), lax.axis_index("pz")
    member = row * count_pz + place
    half_points = planes * groups

    def remote(source, target, send_sem, recv_sem, half, to_member):
        return pltpu.make_async_remote_copy(
            src_ref=source,
            dst_ref=target,
            send_sem=send_sem,
            recv_sem=recv_sem,
            device_id={"tm": half, "py": to_member // count_pz, "pz": lax.rem(to_member, count_pz)},
            device_id_type=pl.DeviceIdType.MESH,
        )

    count_py = lax.axis_size("py")
    early = planes // 2

    def far_first(step):
        to_place = lax.rem(place + count_pz // 2 + step // count_py, count_pz)
        return lax.rem(row + lax.rem(step, count_py), count_py) * count_pz + to_place

    def state_copy(f):
        return remote(state.at[f], earlier.at[f], state_send.at[f], state_recv.at[f], 1, member)

    @pl.when(position == 0)
    def _():
        for f in (1, 2, 0):
            state_copy(f).start()
        earlier[...] = state[...]

    turn = table_refs[0][0:1, :]
    tables_x = (x0[position], x1[position])
    for group, f in enumerate((1, 2, 0)):
        first, count = 2 * group, 2 if f else 1

        @pl.when(position == 1)
        def _():
            state_copy(f).wait_recv()

        parts = [earlier[f, a] for a in range(rows)]
        stacked = jnp.concatenate(
            [
                jnp.concatenate(parts, axis=1),
                jnp.concatenate([pltpu.roll(p, retained // 2, 1) * turn for p in parts], axis=1),
            ],
            axis=0,
        )
        moved = dot3([t[: count * half_points] for t in tables_x], split(stacked))
        for c in range(count):
            flat = spread.at[first + c].reshape(half_points * rows, retained)
            for a in range(rows):
                flat[pl.ds(a, half_points, stride=rows), :] = moved[
                    c * half_points : (c + 1) * half_points, a * retained : (a + 1) * retained
                ]
        recv[first : first + count, :, member] = spread[first : first + count, :, member]

        batches = [(group, 0, planes)] if f else [(group, 0, early), (group + 1, early, planes)]
        for batch, start, stop in batches:

            def push(step, carry, first=first, count=count, batch=batch, start=start, stop=stop):
                to_member = far_first(step)
                fields, span = pl.ds(first, count), pl.ds(start, stop - start)

                @pl.when(to_member != member)
                def _():
                    remote(
                        spread.at[fields, span, to_member],
                        recv.at[fields, span, member],
                        field_send,
                        field_recv.at[batch],
                        position,
                        to_member,
                    ).start()

                return carry

            lax.fori_loop(0, groups, push, 0)

    def await_fields(batch, first, count, start, stop):
        some = recv.at[pl.ds(first, count), pl.ds(start, stop - start), pl.ds(0, groups - 1)]
        remote(some, some, field_send, field_recv.at[batch], position, member).wait_recv()

    await_fields(0, 0, 2, 0, planes)
    await_fields(1, 2, 2, 0, planes)
    await_fields(2, 4, 1, 0, early)

    tables = [ref[...] for ref in table_refs]

    def plane(p, carry):
        @pl.when(p == early)
        def _():
            await_fields(3, 4, 1, early, planes)

        v1, d1, v2, d2, v0 = [recv[f, p].reshape(groups * rows, retained) for f in range(5)]
        for f, values in enumerate(plane_math([v0, v1, v2, d1, d2], tables)):
            result[p, :, f] = values.reshape(groups, rows, retained)

        def push(step, carry):
            to_member = far_first(step)

            @pl.when(jnp.logical_or(position == 0, to_member != member))
            def _():
                remote(
                    result.at[p, to_member],
                    out.at[position, p, member],
                    back_send,
                    back_recv,
                    1,
                    to_member,
                ).start()

            return carry

        lax.fori_loop(0, groups, push, 0)

        @pl.when(position == 1)
        def _():
            pltpu.make_async_copy(result.at[p, member], out.at[1, p, member], back_recv).start()

        return carry

    lax.fori_loop(0, planes, plane, 0)

    some = spread.at[:, :, pl.ds(0, groups - 1)]
    remote(some, some, field_send, field_recv.at[0], position, member).wait_send()

    @pl.when(position == 0)
    def _():
        for f in range(3):
            state_copy(f).wait_send()
        remote(result, result, back_send, back_recv, 1, member).wait_send()

    @pl.when(position == 1)
    def _():
        some = result.at[:, pl.ds(0, groups - 1)]
        remote(some, some, back_send, back_recv, 1, member).wait_send()
        remote(out, out, back_send, back_recv, 1, member).wait_recv()


def helped_advance(state, wavegrid, groups, halves):
    wave_x, wave_y, wave_z = wavegrid
    retained = state.shape[-1]
    rows = state.shape[2]
    extent = 3 * retained // 2
    planes = extent // (groups * halves)
    tables = x_tables(extent, retained, halves) + plane_tables(extent, retained, groups)
    vmem = pl.BlockSpec(memory_space=pltpu.VMEM)
    turned_state = jnp.swapaxes(state, 1, 2)
    arrived, earlier = pl.pallas_call(
        step_kernel,
        in_specs=[vmem] * (1 + len(tables)),
        out_specs=[pl.BlockSpec(memory_space=pl.ANY), vmem],
        out_shape=[
            jax.ShapeDtypeStruct((halves, planes, groups, 3, rows, retained), jnp.float32),
            jax.ShapeDtypeStruct(turned_state.shape, jnp.float32),
        ],
        scratch_shapes=[
            pltpu.VMEM((5, planes, groups, rows, retained), jnp.float32),
            pltpu.VMEM((5, planes, groups, rows, retained), jnp.float32),
            pltpu.VMEM((planes, groups, 3, rows, retained), jnp.float32),
            pltpu.SemaphoreType.DMA((3,)),
            pltpu.SemaphoreType.DMA((3,)),
            pltpu.SemaphoreType.DMA,
            pltpu.SemaphoreType.DMA((4,)),
            pltpu.SemaphoreType.DMA,
            pltpu.SemaphoreType.DMA,
        ],
        compiler_params=pltpu.CompilerParams(
            has_side_effects=True, vmem_limit_bytes=56 * 1024 * 1024
        ),
        name="step",
    )(turned_state, *tables)
    earlier = jnp.swapaxes(earlier, 1, 2)
    arrived = arrived.reshape(extent, 3, rows, retained)
    cosine, sine = trig_table(wave_table(retained), np.arange(extent), extent)
    forward_x = np.concatenate([cosine, -sine], axis=1) * (math.sqrt(retained) / extent)
    both = jnp.concatenate([arrived, rotate(arrived)], axis=0)
    nonlinear = jnp.einsum(
        "kx,xfar->fkar", jnp.asarray(forward_x, jnp.float32), both, precision=lax.Precision.HIGH
    )
    squared = wave_x * wave_x + wave_y * wave_y + wave_z * wave_z
    damping = jnp.exp(-viscosity * time_step * squared)
    return damping * project(earlier + time_step * nonlinear, wavegrid)


def shards(start_states):
    count_py = lax.axis_size("py")
    count_pz = lax.axis_size("pz")
    groups = count_py * count_pz
    member = lax.axis_index("py") * count_pz + lax.axis_index("pz")
    layout = (count_py, count_pz, groups, member)
    position = lax.axis_index("tm")
    slices = lax.axis_size("tm")
    retained = start_states.shape[-1]
    stored = start_states.reshape(3, retained, start_states.shape[3], retained)
    spectral_state = project(stored, wave_grid(retained, layout))
    if slices == 2:
        earlier_end = helped_advance(
            spectral_state, wave_grid(retained, layout), groups, slices
        )
        result = jnp.where(position == 0, spectral_state, earlier_end)
        return result.reshape(1, result.shape[0], retained, result.shape[2], 1, retained)
    fine_end = advance(spectral_state, "fine", layout)
    coarse_start = restrict(spectral_state, M, groups)
    coarse_next = advance(coarse_start, "coarse", layout)
    fine_low = restrict(fine_end, M, groups)
    correction = fine_low - coarse_next

    def relay(chained):
        return shifted(chained, "tm", 1)

    current = jnp.where(position == 1, relay(fine_low), coarse_start)

    def sweep_turn(turn_index, current):
        candidate = advance(current, "coarse", layout) + correction
        arrived = relay(candidate)
        return jnp.where(position == turn_index + 1, arrived, current)

    current = lax.fori_loop(1, slices - 1, sweep_turn, current)
    upper_band = fine_end - prolong(fine_low, retained, groups)
    previous = shifted(upper_band, "tm", 1)
    updated = prolong(current, retained, groups) + previous
    result = jnp.where(position == 0, spectral_state, updated)
    return result.reshape(1, result.shape[0], retained, result.shape[2], 1, retained)


def solution(mesh):
    in_specs = (P("tm", None, None, None, ("py", "pz"), None),)
    out_specs = P("tm", None, None, None, ("py", "pz"), None)
    return jax.shard_map(shards, mesh=mesh, in_specs=in_specs, out_specs=out_specs, check_vma=False)
```

profile of v0, /device:TPU:3, one launch (start us, length us, event | category | flops | bytes accessed | tf_op | source)
XLA Modules:
  0.0 113.8 jit_solution(6751539808886253336)
XLA Ops:
  0.0 0.1 broadcast_add_fusion
  0.1 2.4 %fusion.18 = (f32[1,1,128,8,1,128]{5,4,3,2,1,0:T(1,128)S(1)}, f32[1,1,128,8,1,128]{5,4,3,2,1,0:T(1,128)S(1)}, f32[1,1,128,8,1,128]{5,4,3,2,1,0:T(1,128)S(1)}) fusion(f32[1,3,128,8,1,128]{5,4,3,2,1,0:T(1,128)} %param.14), kind=kLoop, calls=%fused_computation.41 | loop fusion | bytes 3145728 | tf_op jit(solution)/shard_map/slice | solution.py:169
  2.5 0.0 copy-start
  2.6 0.0 copy-start.2
  2.6 0.0 copy-start.4
  2.6 0.5 bitcast_subtract_fusion.2
  3.1 0.3 copy-done
  3.3 0.2 copy-done.2
  3.5 0.2 copy-done.4
  3.7 1.3 %maximum_bitcast_fusion.refs_0_ = f32[3,8,128,128]{3,2,1,0:T(8,128)} fusion(f32[1,128,8,128]{3,1,2,0:T(8,128)S(1)} %get-tuple-element.16, f32[1,128,8,128]{3,1,2,0:T(8,128)S(1)} %get-tuple-element.17, f32[1,128,8,128]{3,1,2,0:T(8,128)S(1)} %get-tuple-element.15), kind=kLoop, calls=%fused_computation.8 | loop fusion | flops 786432 | bytes 3145728 | tf_op jit(solution)/shard_map/transpose | solution.py:489
  5.0 94.9 %step.1 = (f32[2,6,16,3,8,128]{5,4,3,2,1,0:T(8,128)}, f32[3,8,128,128]{3,2,1,0:T(8,128)}) custom-call(f32[3,8,128,128]{3,2,1,0:T(8,128)} %maximum_bitcast_fusion.refs_0_, bf16[2,192,256]{2,1,0:T(8,128)(2,1)} %constant.76.clone.refs_1_, bf16[2,192,256]{2,1,0:T(8,128)(2,1)} %constant.77.clone.refs_2_, f32[8,128]{1,0:T(8,128)} %constant.78.clone.refs_3_, ...), custom_call_target="tpu_custom_call" | custom-call | tf_op jit(solution)/shard_map/step/pallas_call | solution.py:490
  99.9 2.4 %copy.20 = f32[192,3,8,128]{0,3,2,1:T(8,128)S(1)} copy(f32[192,3,8,128]{3,2,1,0:T(8,128)} %bitcast.54) | data formatting | bytes 4718592 | tf_op jit(solution)/shard_map/reshape | solution.py:515
  102.3 0.0 copy-start.6
  102.3 0.0 copy-start.7
  102.3 0.2 slice_negate_fusion
  102.6 1.2 %copy-done.6 = f32[3,8,128,128]{3,2,1,0:T(8,128)S(1)} copy-done((f32[3,8,128,128]{3,2,1,0:T(8,128)S(1)}, f32[3,8,128,128]{3,2,1,0:T(8,128)}, u32[]{:S(2)}) %copy-start.6) | copy-done | bytes 1572888
  103.7 0.0 copy-done.7
  103.7 2.9 %bitcast_add_fusion = f32[3,128,8,128]{3,1,2,0:T(8,128)S(1)} fusion(f32[3,8,128,128]{3,2,1,0:T(8,128)S(1)} %copy-done.6, f32[128,384,1,1]{1,0,3,2:T(8,128)S(1)} %copy-done.7, f32[192,3,8,64]{0,3,2,1:T(8,128)S(1)} %get-tuple-element.12, f32[192,3,8,64]{0,3,2,1:T(8,128)S(1)} %get-tuple-element.11, f32[192,3,8,128]{0,3,2,1:T(8,128)S(1)} %copy.20), kind=kOutput, calls=%fused_computation.10 | convolution fusion | flops 909115392 | bytes 8060928 | tf_op jit(solution)/shard_map/kx,xfar->fkar/dot_general | solution.py:519
  106.6 0.3 subtract_bitcast_fusion.2
  106.9 0.0 copy-start.1
  106.9 0.0 copy-start.3
  106.9 0.0 copy-start.5
  106.9 0.2 subtract_bitcast_fusion.1
  107.1 0.9 copy-done.1
  108.0 0.2 copy-done.3
  108.1 0.2 copy-done.5
  108.3 1.3 %multiply_subtract_fusion.2 = (f32[1,1,128,8,1,128]{5,2,3,4,1,0:T(8,128)S(1)}, f32[1,1,128,8,1,128]{5,2,3,4,1,0:T(8,128)S(1)}, f32[1,1,128,8,1,128]{5,2,3,4,1,0:T(8,128)}) fusion(f32[1,1,128,8,1,128]{5,4,3,2,1,0:T(1,128)S(1)} %copy-done.1, f32[128]{0:T(128)S(1)} %get-tuple-element.25, f32[128]{0:T(128)S(1)} %fusion.15, f32[128,8]{0,1:T(8,128)S(1)} %broadcast_add_fusion, ...), kind=kLoop, calls=%fused_computation.28 | loop fusion | flops 1835008 | bytes 3151392 | tf_op jit(solution)/shard_map/sub | solution.py:169
  109.6 0.2 multiply_exponential_fusion
  109.8 1.3 %maximum_select_fusion = f32[1,3,128,8,1,128]{5,2,3,4,1,0:T(8,128)S(1)} fusion(f32[1,1,128,8,1,128]{5,2,3,4,1,0:T(8,128)S(1)} %get-tuple-element.19, f32[1,1,128,8,1,128]{5,2,3,4,1,0:T(8,128)} %get-tuple-element.20, f32[1,1,128,8,1,128]{5,2,3,4,1,0:T(8,128)S(1)} %get-tuple-element.18, f32[1,1,128,8,1,128]{5,2,3,4,1,0:T(8,128)S(1)} %get-tuple-element.14, ...), kind=kLoop, calls=%fused_computation.7 | loop fusion | flops 2359296 | bytes 5242881 | tf_op jit(solution)/shard_map/jit(_where)/select_n | solution.py:542
  111.1 2.8 %copy.22 = f32[1,3,128,8,1,128]{5,4,3,2,1,0:T(1,128)} copy(f32[1,3,128,8,1,128]{5,2,3,4,1,0:T(8,128)S(1)} %maximum_select_fusion) | data formatting | bytes 3145728 | tf_op jit(solution)/shard_map/jit(_where)/select_n | solution.py:542
  (5 shorter events, 0.0 us)
Async XLA Ops:
  2.5 0.8 copy-start
  2.6 1.0 copy-start.2
  2.6 1.2 %copy-start.4 = (f32[1,1,128,8,1,128]{5,4,3,2,1,0:T(1,128)}, f32[1,1,128,8,1,128]{5,4,3,2,1,0:T(1,128)S(1)}, u32[]{:S(2)}) copy-start(f32[1,1,128,8,1,128]{5,4,3,2,1,0:T(1,128)S(1)} %get-tuple-element.23) | copy-start | bytes 1572868
  102.3 1.4 %copy-start.6 = (f32[3,8,128,128]{3,2,1,0:T(8,128)S(1)}, f32[3,8,128,128]{3,2,1,0:T(8,128)}, u32[]{:S(2)}) copy-start(f32[3,8,128,128]{3,2,1,0:T(8,128)} %get-tuple-element.7) | copy-start | bytes 4718596
  102.3 1.4 %copy-start.7 = (f32[128,384,1,1]{1,0,3,2:T(8,128)S(1)}, f32[128,384,1,1]{1,0,3,2:T(8,128)}, u32[]{:S(2)}) copy-start(f32[128,384,1,1]{1,0,3,2:T(8,128)} %constant.90) | copy-start | bytes 589828
  106.9 1.0 copy-start.1
  106.9 1.2 %copy-start.3 = (f32[1,1,128,8,1,128]{5,4,3,2,1,0:T(1,128)S(1)}, f32[1,1,128,8,1,128]{5,4,3,2,1,0:T(1,128)}, u32[]{:S(2)}) copy-start(f32[1,1,128,8,1,128]{5,4,3,2,1,0:T(1,128)} %copy-done.2) | copy-start | bytes 1572868
  106.9 1.3 %copy-start.5 = (f32[1,1,128,8,1,128]{5,4,3,2,1,0:T(1,128)S(1)}, f32[1,1,128,8,1,128]{5,4,3,2,1,0:T(1,128)}, u32[]{:S(2)}) copy-start(f32[1,1,128,8,1,128]{5,4,3,2,1,0:T(1,128)} %copy-done.4) | copy-start | bytes 1572868
where the time goes:
time: 115 us; the launch traced here: 114 us
  Pallas kernels  94.9 us (83%)
  local copies, waits for them, and re-layouts  10.6 us (9%)
  other arithmetic  5.29 us (5%)
  matrix products  2.9 us (3%)
    pallas_call x1, Pallas kernels, helped_advance(): pl.pallas_call(step_kernel, in_specs=[vmem] * (1 + len(tables)), out_spec...  94.9 us
    unnamed x16, local copies, waits for them, and re-layouts  3.03 us
    dot_general x1, matrix products, helped_advance(): jnp.einsum('kx,xfar->fkar', jnp.asarray(forward_x, jnp.float32), both, pr...  2.9 us
    select_n x1, local copies, waits for them, and re-layouts, shards(): result = jnp.where(position == 0, spectral_state, earlier_end)  2.76 us
    slice x1, local copies, waits for them, and re-layouts, project(): coeffs[0] - wave_x * divergence  2.44 us
    reshape x1, local copies, waits for them, and re-layouts, helped_advance(): arrived = arrived.reshape(extent, 3, rows, retained)  2.39 us

commit v1 on v0

--- a/solution.py
+++ b/solution.py
@@ -264,24 +264,41 @@
     return table * weight, table.T * (math.sqrt(retained) / extent)
 
 
-def plane_tables(extent, retained, groups):
+def wave_order(retained, count_py, count_pz):
+    groups = count_py * count_pz
+    rows, near = retained // groups, count_pz // 2
+    side, band, line, z_low, inner = np.meshgrid(
+        np.arange(2),
+        np.arange(2),
+        np.arange(count_py),
+        np.arange(near),
+        np.arange(rows // 2),
+        indexing="ij",
+    )
+    owner = line * count_pz + side * near + z_low
+    return ((band * (rows // 2) + inner) * groups + owner).reshape(-1)
+
+
+def plane_tables(extent, retained, count_py, count_pz):
+    groups = count_py * count_pz
     rows = retained // groups
     places = np.arange(retained)
-    wave_y = wave_table(retained)[places % rows * groups + places // rows]
-    cosine, sine = trig_table(np.arange(extent), wave_y, extent)
+    wave_in = wave_table(retained)[wave_order(retained, count_py, count_pz)]
+    wave_out = wave_table(retained)[places % rows * groups + places // rows]
+    cosine, sine = trig_table(np.arange(extent), wave_in, extent)
     inverse_y = np.concatenate([cosine, sine], axis=1) * retained ** (-0.5)
-    forward_y = np.concatenate([cosine.T, -sine.T], axis=1) * (math.sqrt(retained) / extent)
+    cosine, sine = trig_table(wave_out, np.arange(extent), extent)
+    forward_y = np.concatenate([cosine, -sine], axis=1) * (math.sqrt(retained) / extent)
     inverse_last, forward_last = z_tables(extent, retained)
     halfway = retained // 2
-    turn = np.where(places < halfway, -1.0, 1.0)
-    wave_z = (places % halfway).astype(np.float32)
     lanes = np.zeros((8, retained), np.float32)
-    lanes[0], lanes[1] = turn, wave_z
-    column = np.broadcast_to(wave_y[:, None], (retained, retained)).astype(np.float32)
+    lanes[0] = np.where(places < halfway, -1.0, 1.0)
+    lanes[1] = places % halfway
+    column = np.broadcast_to(wave_in[:, None], (retained, retained)).astype(np.float32)
     tables = [lanes, column]
     for table in (inverse_y, inverse_last, forward_last, forward_y):
         tables += split_table(table)
-    return [jnp.asarray(t) for t in tables]
+    return tables
 
 
 def plane_math(fields, tables):
@@ -320,208 +337,447 @@
     return [result[:, f * retained : (f + 1) * retained] for f in range(3)]
 
 
-def x_tables(extent, retained, halves):
+def point_place(position, side, spot, plane, near_group, planes):
+    return ((position * 2 + side) * near_group + spot) * planes + plane
+
+
+def x_tables(extent, retained, count_py, count_pz, halves):
+    near = count_pz // 2
+    near_group = count_py * near
+    planes = extent // (2 * near_group * halves)
     wave_x = wave_table(retained)
-    cosine, sine = trig_table(np.arange(extent), wave_x, extent)
-    values = np.concatenate([cosine, sine], axis=1)
-    slopes = np.concatenate([-sine * wave_x, cosine * wave_x], axis=1)
-    per_half = [table.reshape(halves, extent // halves, -1) for table in (values, slopes)]
-    table = np.concatenate(per_half, axis=1) * retained ** (-0.5)
-    return [jnp.asarray(t) for t in split_table(table)]
+    plane, spot = np.meshgrid(np.arange(planes), np.arange(near_group), indexing="ij")
+    inverse = []
+    for position in range(halves):
+        for side in range(2):
+            points = point_place(position, side, spot, plane, near_group, planes).reshape(-1)
+            cosine, sine = trig_table(points, wave_x, extent)
+            values = np.concatenate([cosine, sine], axis=1)
+            slopes = np.concatenate([-sine * wave_x, cosine * wave_x], axis=1)
+            inverse.append(np.concatenate([values, slopes], axis=0))
+    inverse = np.stack(inverse) * retained ** (-0.5)
+    plane, position, line, side, z_low = np.meshgrid(
+        np.arange(planes),
+        np.arange(halves),
+        np.arange(count_py),
+        np.arange(2),
+        np.arange(near),
+        indexing="ij",
+    )
+    points = point_place(position, side, line * near + z_low, plane, near_group, planes)
+    points = points.reshape(planes, -1)
+    early = planes - 2
+    forward = []
+    for some in (points[:early].reshape(-1), points[early:].reshape(-1)):
+        cosine, sine = trig_table(wave_x, some, extent)
+        forward.append(np.concatenate([cosine, -sine], axis=1) * (math.sqrt(retained) / extent))
+    column = np.broadcast_to(wave_x[:, None], (retained, retained)).astype(np.float32)
+    tables = [column]
+    for table in [inverse] + forward:
+        tables += split_table(table)
+    return tables
 
 
 def step_kernel(*refs):
-    state, x0, x1 = refs[:3]
-    table_refs = refs[3:13]
-    out, earlier = refs[13:15]
-    spread, recv, result = refs[15:18]
-    state_send, state_recv, field_send, field_recv, back_send, back_recv = refs[18:]
-    _, planes, groups, rows, retained = spread.shape
-    count_pz = lax.axis_size("pz")
+    stored = refs[0]
+    wave_x_ref, xi0, xi1, fa0, fa1, fb0, fb1 = refs[1:8]
+    plane_refs = refs[8:18]
+    out = refs[18]
+    raw, modes, spread, recv, result, arrived, partial_sum = refs[19:26]
+    load_sem, mode_send, own_recv, pair_recv, field_send, field_recv, back_send, back_recv = refs[26:]
+
+    _, retained, rows, _ = stored.shape
+    planes, groups = result.shape[:2]
+    halves = arrived.shape[1] // groups
+    count_py, count_pz = lax.axis_size("py"), lax.axis_size("pz")
+    near = count_pz // 2
+    near_group = count_py * near
+    band = rows // 2
+    pairs = planes // 2
+    early = planes - 2
     position = lax.axis_index("tm")
     row, place = lax.axis_index("py"), lax.axis_index("pz")
+    side, z_low = place // near, lax.rem(place, near)
+    spot = row * near + z_low
     member = row * count_pz + place
-    half_points = planes * groups
-
-    def remote(source, target, send_sem, recv_sem, half, to_member):
+    pair_place = lax.rem(place + near, count_pz)
+    pair_member = row * count_pz + pair_place
+    lanes = plane_refs[0]
+    turn, wave_z = lanes[0:1, :], lanes[1:2, :]
+
+    def remote(source, target, send_sem, recv_sem, device):
         return pltpu.make_async_remote_copy(
             src_ref=source,
             dst_ref=target,
             send_sem=send_sem,
             recv_sem=recv_sem,
-            device_id={"tm": half, "py": to_member // count_pz, "pz": lax.rem(to_member, count_pz)},
+            device_id=device,
             device_id_type=pl.DeviceIdType.MESH,
         )
 
-    count_py = lax.axis_size("py")
-    early = planes // 2
-
-    def far_first(step):
-        to_place = lax.rem(place + count_pz // 2 + step // count_py, count_pz)
-        return lax.rem(row + lax.rem(step, count_py), count_py) * count_pz + to_place
-
-    def state_copy(f):
-        return remote(state.at[f], earlier.at[f], state_send.at[f], state_recv.at[f], 1, member)
+    def device(half, line, z_place):
+        return {"tm": half, "py": line, "pz": z_place}
+
+    across = device(1 - position, row, place)
+    beside = device(position, row, pair_place)
+
+    def turned(values):
+        return pltpu.roll(values, retained // 2, 1) * turn
+
+    def wave_y_of(a, owner):
+        place_y = a * groups + owner
+        return jnp.where(place_y < retained // 2, place_y, place_y - retained).astype(jnp.float32)
+
+    def strided(ref, f, a):
+        return ref.at[f].reshape(retained * rows, retained), pl.ds(a, retained, stride=rows)
 
     @pl.when(position == 0)
     def _():
+        pltpu.make_async_copy(stored, raw, load_sem).start()
+
+    barrier = pltpu.get_barrier_semaphore()
+    total = halves * groups
+    me = position * groups + member
+
+    def greet(step, carry):
+        other = lax.rem(me + step, total)
+        owner = lax.rem(other, groups)
+        pl.semaphore_signal(
+            barrier,
+            inc=1,
+            device_id=device(other // groups, owner // count_pz, lax.rem(owner, count_pz)),
+            device_id_type=pl.DeviceIdType.MESH,
+        )
+        return carry
+
+    lax.fori_loop(1, total, greet, 0)
+
+    def project(values, wave_y):
+        wave_x = wave_x_ref[...]
+        squared = wave_x * wave_x + (wave_y * wave_y + wave_z * wave_z)
+        divergence = (wave_x * values[0] + wave_y * values[1] + wave_z * values[2]) / jnp.maximum(
+            squared, 1.0
+        )
+        projected = [
+            values[0] - wave_x * divergence,
+            values[1] - wave_y * divergence,
+            values[2] - wave_z * divergence,
+        ]
+        return projected, squared
+
+    def flat_squares(wave_y):
+        squares = wave_y * wave_y + wave_z * wave_z
+        return squares < 0.5, 1.0 / jnp.maximum(squares, 1.0)
+
+    @pl.when(position == 0)
+    def _():
+        pltpu.make_async_copy(stored, raw, load_sem).wait()
+
+        def first(a, carry):
+            wave_y = wave_y_of(a, member)
+            values = []
+            for f in range(3):
+                view, rows_of = strided(raw, f, a)
+                values.append(view[rows_of, :])
+            values, _ = project(values, wave_y)
+            for f in range(3):
+                view, rows_of = strided(out, f, a)
+                view[rows_of, :] = values[f]
+            still, inverse = flat_squares(wave_y)
+            turning = (wave_y * values[2] - wave_z * values[1]) * inverse
+            modes[0, a, 0:retained, :] = jnp.where(still, values[1], values[0])
+            modes[0, a, retained : 2 * retained, :] = jnp.where(still, values[2], turning)
+            modes[0, a, 2 * retained : 2 * retained + 8, :] = values[0][0:8]
+            return carry
+
+        lax.fori_loop(0, rows, first, 0)
+
+    pl.semaphore_wait(barrier, total - 1)
+
+    def rebuild(slot, a, owner):
+        wave_y = wave_y_of(a, owner)
+        wave_x = wave_x_ref[...]
+        still, inverse = flat_squares(wave_y)
+        first = modes[slot, a, 0:retained, :]
+        second = modes[slot, a, retained : 2 * retained, :]
+        mean = modes[slot, a, 2 * retained : 2 * retained + 1, :]
+        pushed = wave_x * first
+        v0 = jnp.where(still, jnp.where(wave_x == 0.0, mean, 0.0), first)
+        v1 = jnp.where(still, first, -(wave_y * inverse) * pushed - wave_z * second)
+        v2 = jnp.where(still, second, -(wave_z * inverse) * pushed + wave_y * second)
+        return v0, v1, v2
+
+    def own_copy(a):
+        return remote(modes.at[0, a], modes.at[0, a], mode_send, own_recv.at[a], across)
+
+    def pair_copy(a):
+        return remote(modes.at[0, a], modes.at[1, a], mode_send, pair_recv.at[a], beside)
+
+    def relay_copy(a):
+        return remote(modes.at[1, a], modes.at[1, a], mode_send, pair_recv.at[a], across)
+
+    def each(start, stop, do):
+        def body(a, carry):
+            do(a)
+            return carry
+
+        lax.fori_loop(start, stop, body, 0)
+
+    def transform(step, slot, high, owner, slot_side):
+        quadrant = position * 2 + side
+        tables = (xi0[quadrant], xi1[quadrant])
+        fields = [rebuild(slot, high * band + a, owner) for a in range(band)]
+        points = planes * near_group
         for f in (1, 2, 0):
-            state_copy(f).start()
-        earlier[...] = state[...]
-
-    turn = table_refs[0][0:1, :]
-    tables_x = (x0[position], x1[position])
-    for group, f in enumerate((1, 2, 0)):
-        first, count = 2 * group, 2 if f else 1
-
-        @pl.when(position == 1)
-        def _():
-            state_copy(f).wait_recv()
-
-        parts = [earlier[f, a] for a in range(rows)]
-        stacked = jnp.concatenate(
-            [
-                jnp.concatenate(parts, axis=1),
-                jnp.concatenate([pltpu.roll(p, retained // 2, 1) * turn for p in parts], axis=1),
-            ],
-            axis=0,
-        )
-        moved = dot3([t[: count * half_points] for t in tables_x], split(stacked))
-        for c in range(count):
-            flat = spread.at[first + c].reshape(half_points * rows, retained)
-            for a in range(rows):
-                flat[pl.ds(a, half_points, stride=rows), :] = moved[
-                    c * half_points : (c + 1) * half_points, a * retained : (a + 1) * retained
-                ]
-        recv[first : first + count, :, member] = spread[first : first + count, :, member]
-
-        batches = [(group, 0, planes)] if f else [(group, 0, early), (group + 1, early, planes)]
-        for batch, start, stop in batches:
-
-            def push(step, carry, first=first, count=count, batch=batch, start=start, stop=stop):
-                to_member = far_first(step)
-                fields, span = pl.ds(first, count), pl.ds(start, stop - start)
-
-                @pl.when(to_member != member)
+            parts = [fields[a][f] for a in range(band)]
+            stacked = jnp.concatenate(
+                [
+                    jnp.concatenate(parts, axis=1),
+                    jnp.concatenate([turned(p) for p in parts], axis=1),
+                ],
+                axis=0,
+            )
+            count = 2 if f else 1
+            moved = dot3([t[: count * points] for t in tables], split(stacked))
+            for p in range(planes):
+                for c in range(count):
+                    if f:
+                        group, offset = p // 2 * 5 + p % 2 * 2 + f - 1, c
+                    else:
+                        group, offset = p // 2 * 5 + 4, p % 2
+                    view = spread.at[step, group].reshape(near_group * rows, retained)
+                    top = c * points + p * near_group
+                    for a in range(band):
+                        view[pl.ds(2 * a + offset, near_group, stride=rows), :] = moved[
+                            top : top + near_group, a * retained : (a + 1) * retained
+                        ]
+        chunk = slot_side * 2 + high
+        slots = chunk * near_group
+        recv[:, slots + spot] = spread[step, :, spot]
+        spans = [(step, 0, 5 * pairs)]
+        if step == 3:
+            spans = [(step + k, 5 * k, 5) for k in range(pairs)]
+        for semaphore, start, count in spans:
+
+            def push(turn_index, carry, semaphore=semaphore, start=start, count=count):
+                other = lax.rem(spot + near_group - turn_index, near_group)
+                remote(
+                    spread.at[step, pl.ds(start, count), other],
+                    recv.at[pl.ds(start, count), slots + spot],
+                    field_send,
+                    field_recv.at[semaphore],
+                    device(position, other // near, side * near + lax.rem(other, near)),
+                ).start()
+                return carry
+
+            lax.fori_loop(1, near_group, push, 0)
+
+    @pl.when(position == 0)
+    def _():
+        each(band, rows, lambda a: own_copy(a).start())
+        each(0, band, lambda a: pair_copy(a).start())
+        each(0, band, lambda a: own_copy(a).start())
+
+    @pl.when(position == 1)
+    def _():
+        def relay(a):
+            own_copy(a).wait_recv()
+            pair_copy(a).start()
+
+        each(band, rows, relay)
+
+    transform(0, 0, 1, member, side)
+
+    def take_pair(a):
+        pair_copy(a).wait_recv()
+        relay_copy(a).start()
+
+    @pl.when(position == 1)
+    def _():
+        def weave(a):
+            take_pair(a + band)
+            own_copy(a).wait_recv()
+
+        each(0, band - 1, weave)
+        own_copy(band - 1).wait_recv()
+
+    transform(1, 0, 0, member, side)
+
+    @pl.when(position == 0)
+    def _():
+        each(0, band, take_pair)
+
+    @pl.when(position == 1)
+    def _():
+        take_pair(rows - 1)
+
+    transform(2, 1, position, pair_member, 1 - side)
+
+    @pl.when(position == 0)
+    def _():
+        each(band, rows, lambda a: relay_copy(a).wait_recv())
+
+    @pl.when(position == 1)
+    def _():
+        each(0, band, lambda a: relay_copy(a).wait_recv())
+
+    transform(3, 1, 1 - position, pair_member, 1 - side)
+
+    def await_fields(semaphore, start, count):
+        some = recv.at[pl.ds(start, count), pl.ds(0, near_group - 1)]
+        remote(some, some, field_send, field_recv.at[semaphore], beside).wait_recv()
+
+    for step in range(3):
+        await_fields(step, 0, 5 * pairs)
+
+    tables = [ref[...] for ref in plane_refs]
+
+    def plane_pair(k, carry):
+        await_fields(3 + k, 5 * k, 5)
+
+        def plane(odd, carry):
+            p = 2 * k + odd
+
+            def field(group, offset):
+                view = recv.at[5 * k + group].reshape(4 * near_group * rows, retained)
+                return view[pl.ds(offset, retained, stride=2), :]
+
+            v1, d1 = field(2 * odd, 0), field(2 * odd, 1)
+            v2, d2 = field(2 * odd + 1, 0), field(2 * odd + 1, 1)
+            v0 = field(4, odd)
+            for f, values in enumerate(plane_math([v0, v1, v2, d1, d2], tables)):
+                result[p, :, f] = values.reshape(groups, rows, retained)
+
+            def push(turn_index, carry):
+                to_place = lax.rem(place + near + turn_index // count_py, count_pz)
+                to_row = lax.rem(row + turn_index, count_py)
+                to_member = to_row * count_pz + to_place
+
+                @pl.when(jnp.logical_or(position == 0, to_member != member))
                 def _():
                     remote(
-                        spread.at[fields, span, to_member],
-                        recv.at[fields, span, member],
-                        field_send,
-                        field_recv.at[batch],
-                        position,
-                        to_member,
+                        result.at[p, to_member],
+                        arrived.at[p, position * groups + member],
+                        back_send,
+                        back_recv.at[p],
+                        device(1, to_row, to_place),
                     ).start()
 
                 return carry
 
             lax.fori_loop(0, groups, push, 0)
 
-    def await_fields(batch, first, count, start, stop):
-        some = recv.at[pl.ds(first, count), pl.ds(start, stop - start), pl.ds(0, groups - 1)]
-        remote(some, some, field_send, field_recv.at[batch], position, member).wait_recv()
-
-    await_fields(0, 0, 2, 0, planes)
-    await_fields(1, 2, 2, 0, planes)
-    await_fields(2, 4, 1, 0, early)
-
-    tables = [ref[...] for ref in table_refs]
-
-    def plane(p, carry):
-        @pl.when(p == early)
-        def _():
-            await_fields(3, 4, 1, early, planes)
-
-        v1, d1, v2, d2, v0 = [recv[f, p].reshape(groups * rows, retained) for f in range(5)]
-        for f, values in enumerate(plane_math([v0, v1, v2, d1, d2], tables)):
-            result[p, :, f] = values.reshape(groups, rows, retained)
-
-        def push(step, carry):
-            to_member = far_first(step)
-
-            @pl.when(jnp.logical_or(position == 0, to_member != member))
+            @pl.when(position == 1)
             def _():
-                remote(
-                    result.at[p, to_member],
-                    out.at[position, p, member],
-                    back_send,
-                    back_recv,
-                    1,
-                    to_member,
-                ).start()
+                arrived[p, groups + member] = result[p, member]
 
             return carry
 
-        lax.fori_loop(0, groups, push, 0)
-
-        @pl.when(position == 1)
-        def _():
-            pltpu.make_async_copy(result.at[p, member], out.at[1, p, member], back_recv).start()
-
-        return carry
-
-    lax.fori_loop(0, planes, plane, 0)
-
-    some = spread.at[:, :, pl.ds(0, groups - 1)]
-    remote(some, some, field_send, field_recv.at[0], position, member).wait_send()
+        return lax.fori_loop(0, 2, plane, carry)
+
+    lax.fori_loop(0, pairs, plane_pair, 0)
+
+    def gather(start, count, a):
+        view = arrived.reshape(planes * total * 3 * rows, retained)
+        wide = jnp.concatenate(
+            [
+                view[pl.ds((start * total * 3 + f) * rows + a, count * total, stride=3 * rows), :]
+                for f in range(3)
+            ],
+            axis=1,
+        )
+        back = jnp.concatenate(
+            [
+                turned(wide[:, f * retained : (f + 1) * retained])
+                for f in range(3)
+            ],
+            axis=1,
+        )
+        return split(jnp.concatenate([wide, back], axis=0))
+
+    @pl.when(position == 1)
+    def _():
+        def await_plane(p):
+            some = arrived.at[p, pl.ds(0, total - 1)]
+            remote(some, some, back_send, back_recv.at[p], beside).wait_recv()
+
+        each(0, early, await_plane)
+
+        def begin(a):
+            partial_sum[a] = dot3((fa0[...], fa1[...]), gather(0, early, a))
+
+        each(0, rows, begin)
+        each(early, planes, await_plane)
+
+        def finish(a):
+            change = partial_sum[a] + dot3((fb0[...], fb1[...]), gather(early, planes - early, a))
+            wave_y = wave_y_of(a, member)
+            before = rebuild(0, a, member)
+            values = [
+                before[f] + time_step * change[:, f * retained : (f + 1) * retained]
+                for f in range(3)
+            ]
+            values, squared = project(values, wave_y)
+            damping = jnp.exp((-viscosity * time_step) * squared)
+            for f in range(3):
+                view, rows_of = strided(out, f, a)
+                view[rows_of, :] = damping * values[f]
+
+        each(0, rows, finish)
+
+    some = spread.at[:, :, pl.ds(0, near_group - 1)]
+    remote(some, some, field_send, field_recv.at[0], beside).wait_send()
 
     @pl.when(position == 0)
     def _():
-        for f in range(3):
-            state_copy(f).wait_send()
-        remote(result, result, back_send, back_recv, 1, member).wait_send()
+        remote(modes, modes, mode_send, own_recv.at[0], beside).wait_send()
+        remote(result, result, back_send, back_recv.at[0], beside).wait_send()
 
     @pl.when(position == 1)
     def _():
+        remote(modes.at[0], modes.at[0], mode_send, own_recv.at[0], beside).wait_send()
         some = result.at[:, pl.ds(0, groups - 1)]
-        remote(some, some, back_send, back_recv, 1, member).wait_send()
-        remote(out, out, back_send, back_recv, 1, member).wait_recv()
-
-
-def helped_advance(state, wavegrid, groups, halves):
-    wave_x, wave_y, wave_z = wavegrid
-    retained = state.shape[-1]
-    rows = state.shape[2]
+        remote(some, some, back_send, back_recv.at[0], beside).wait_send()
+
+
+def helped_advance(stored, count_py, count_pz, halves):
+    _, retained, rows, _ = stored.shape
+    groups = count_py * count_pz
     extent = 3 * retained // 2
+    near_group = groups // 2
     planes = extent // (groups * halves)
-    tables = x_tables(extent, retained, halves) + plane_tables(extent, retained, groups)
+    pairs = planes // 2
+    tables = x_tables(extent, retained, count_py, count_pz, halves)
+    tables += plane_tables(extent, retained, count_py, count_pz)
+    tables = [jnp.asarray(table) for table in tables]
     vmem = pl.BlockSpec(memory_space=pltpu.VMEM)
-    turned_state = jnp.swapaxes(state, 1, 2)
-    arrived, earlier = pl.pallas_call(
+    return pl.pallas_call(
         step_kernel,
-        in_specs=[vmem] * (1 + len(tables)),
-        out_specs=[pl.BlockSpec(memory_space=pl.ANY), vmem],
-        out_shape=[
-            jax.ShapeDtypeStruct((halves, planes, groups, 3, rows, retained), jnp.float32),
-            jax.ShapeDtypeStruct(turned_state.shape, jnp.float32),
-        ],
+        in_specs=[pl.BlockSpec(memory_space=pl.ANY)] + [vmem] * len(tables),
+        out_specs=vmem,
+        out_shape=jax.ShapeDtypeStruct(stored.shape, jnp.float32),
         scratch_shapes=[
-            pltpu.VMEM((5, planes, groups, rows, retained), jnp.float32),
-            pltpu.VMEM((5, planes, groups, rows, retained), jnp.float32),
+            pltpu.VMEM(stored.shape, jnp.float32),
+            pltpu.VMEM((2, rows, 2 * retained + 8, retained), jnp.float32),
+            pltpu.VMEM((4, 5 * pairs, near_group, rows, retained), jnp.float32),
+            pltpu.VMEM((5 * pairs, 4 * near_group, rows, retained), jnp.float32),
             pltpu.VMEM((planes, groups, 3, rows, retained), jnp.float32),
-            pltpu.SemaphoreType.DMA((3,)),
-            pltpu.SemaphoreType.DMA((3,)),
-            pltpu.SemaphoreType.DMA,
-            pltpu.SemaphoreType.DMA((4,)),
+            pltpu.VMEM((planes, halves * groups, 3, rows, retained), jnp.float32),
+            pltpu.VMEM((rows, retained, 3 * retained), jnp.float32),
             pltpu.SemaphoreType.DMA,
             pltpu.SemaphoreType.DMA,
+            pltpu.SemaphoreType.DMA((rows,)),
+            pltpu.SemaphoreType.DMA((rows,)),
+            pltpu.SemaphoreType.DMA,
+            pltpu.SemaphoreType.DMA((3 + pairs,)),
+            pltpu.SemaphoreType.DMA,
+            pltpu.SemaphoreType.DMA((planes,)),
         ],
         compiler_params=pltpu.CompilerParams(
-            has_side_effects=True, vmem_limit_bytes=56 * 1024 * 1024
+            has_side_effects=True, collective_id=0, vmem_limit_bytes=56 * 1024 * 1024
         ),
         name="step",
-    )(turned_state, *tables)
-    earlier = jnp.swapaxes(earlier, 1, 2)
-    arrived = arrived.reshape(extent, 3, rows, retained)
-    cosine, sine = trig_table(wave_table(retained), np.arange(extent), extent)
-    forward_x = np.concatenate([cosine, -sine], axis=1) * (math.sqrt(retained) / extent)
-    both = jnp.concatenate([arrived, rotate(arrived)], axis=0)
-    nonlinear = jnp.einsum(
-        "kx,xfar->fkar", jnp.asarray(forward_x, jnp.float32), both, precision=lax.Precision.HIGH
-    )
-    squared = wave_x * wave_x + wave_y * wave_y + wave_z * wave_z
-    damping = jnp.exp(-viscosity * time_step * squared)
-    return damping * project(earlier + time_step * nonlinear, wavegrid)
+    )(stored, *tables)
 
 
 def shards(start_states):
@@ -534,13 +790,10 @@
     slices = lax.axis_size("tm")
     retained = start_states.shape[-1]
     stored = start_states.reshape(3, retained, start_states.shape[3], retained)
+    if slices == 2:
+        result = helped_advance(stored, count_py, count_pz, slices)
+        return result.reshape(1, 3, retained, stored.shape[2], 1, retained)
     spectral_state = project(stored, wave_grid(retained, layout))
-    if slices == 2:
-        earlier_end = helped_advance(
-            spectral_state, wave_grid(retained, layout), groups, slices
-        )
-        result = jnp.where(position == 0, spectral_state, earlier_end)
-        return result.reshape(1, result.shape[0], retained, result.shape[2], 1, retained)
     fine_end = advance(spectral_state, "fine", layout)
     coarse_start = restrict(spectral_state, M, groups)
     coarse_next = advance(coarse_start, "coarse", layout)

time: 115 us -> 94 us (0.82)
  local copies, waits for them, and re-layouts: 10.6 us -> 3.63 us
  Pallas kernels: 94.9 us -> 89.2 us
  other arithmetic: 5.29 us -> 0 us
  matrix products: 2.9 us -> 0 us
    pallas_call x1, Pallas kernels: 94.9 us -> 89.2 us  [helped_advance(): pl.pallas_call(step_kernel, in_specs=[pl.BlockSpec(memory_space=pl.ANY)]...]
    dot_general x1 -> x0, matrix products: 2.9 us -> none  [helped_advance(): jnp.einsum('kx,xfar->fkar', jnp.asarray(forward_x, jnp.float32), both, pr...]
    select_n x1 -> x0, local copies, waits for them, and re-layouts: 2.76 us -> none  [shards(): result = jnp.where(position == 0, spectral_state, earlier_end)]
    slice x1 -> x0, local copies, waits for them, and re-layouts: 2.44 us -> none  [project(): coeffs[0] - wave_x * divergence]
    reshape x1 -> x0, local copies, waits for them, and re-layouts: 2.39 us -> none  [helped_advance(): arrived = arrived.reshape(extent, 3, rows, retained)]
    sub x2 -> x0, other arithmetic: 1.75 us -> none  [project(): coeffs[0] - wave_x * divergence]
    transpose x1 -> x0, other arithmetic: 1.29 us -> none  [helped_advance(): turned_state = jnp.swapaxes(state, 1, 2)]
    select_n x1 -> x0, other arithmetic: 1.28 us -> none  [shards(): result = jnp.where(position == 0, spectral_state, earlier_end)]
where the time goes in v1:
time: 94 us; the launch traced here: 92.9 us
  Pallas kernels  89.2 us (95%)
  local copies, waits for them, and re-layouts  3.63 us (4%)
    pallas_call x1, Pallas kernels, helped_advance(): pl.pallas_call(step_kernel, in_specs=[pl.BlockSpec(memory_space=pl.ANY)]...  89.2 us
    unnamed x1, local copies, waits for them, and re-layouts  3.63 us

profile of v1, /device:TPU:3, one launch (start us, length us, event | category | flops | bytes accessed | tf_op | source)
XLA Modules:
  0.0 92.9 jit_solution(14386482193920435692)
XLA Ops:
  0.0 89.2 %step.1 = f32[3,128,8,128]{3,2,1,0:T(8,128)} custom-call(f32[3,128,8,128]{3,2,1,0:T(8,128)} %bitcast.5, f32[128,128]{1,0:T(8,128)} %constant.34.clone.refs_1_, bf16[4,96,256]{2,1,0:T(8,128)(2,1)} %constant.35.clone.refs_2_, bf16[4,96,256]{2,1,0:T(8,128)(2,1)} %constant.36.clone.refs_3_, bf16[128,256]{1,0:T(8,128)(2,1)} %constant.37.clone.refs_4_, ...), custom_call_target="tpu_custom_call" | custom-call | tf_op jit(solution)/shard_map/step/pallas_call | solution.py:754
  89.2 3.6 %copy.21 = f32[1,3,128,8,1,128]{5,4,3,2,1,0:T(1,128)} copy(f32[1,3,128,8,1,128]{5,4,3,2,1,0:T(1,128)} %bitcast.4) | data formatting | bytes 3145728

commit v2 on v1

--- a/solution.py
+++ b/solution.py
@@ -380,11 +380,14 @@
 
 def step_kernel(*refs):
     stored = refs[0]
-    wave_x_ref, xi0, xi1, fa0, fa1, fb0, fb1 = refs[1:8]
-    plane_refs = refs[8:18]
+    kept_tables = refs[1:18]
     out = refs[18]
-    raw, modes, spread, recv, result, arrived, partial_sum = refs[19:26]
-    load_sem, mode_send, own_recv, pair_recv, field_send, field_recv, back_send, back_recv = refs[26:]
+    loaded = refs[19:36]
+    wave_x_ref, xi0, xi1, fa0, fa1, fb0, fb1 = loaded[:7]
+    plane_refs = loaded[7:]
+    raw, modes, spread, recv, result, arrived, partial_sum = refs[36:43]
+    load_sem, table_sem, mode_send, own_recv, pair_recv = refs[43:48]
+    field_send, field_recv, back_send, back_recv, ready = refs[48:]
 
     _, retained, rows, _ = stored.shape
     planes, groups = result.shape[:2]
@@ -402,8 +405,6 @@
     member = row * count_pz + place
     pair_place = lax.rem(place + near, count_pz)
     pair_member = row * count_pz + pair_place
-    lanes = plane_refs[0]
-    turn, wave_z = lanes[0:1, :], lanes[1:2, :]
 
     def remote(source, target, send_sem, recv_sem, device):
         return pltpu.make_async_remote_copy(
@@ -431,26 +432,37 @@
     def strided(ref, f, a):
         return ref.at[f].reshape(retained * rows, retained), pl.ds(a, retained, stride=rows)
 
+    total = halves * groups
+    barrier = pltpu.get_barrier_semaphore()
+
+    def hello(other):
+        pl.semaphore_signal(
+            barrier, inc=1, device_id=other, device_id_type=pl.DeviceIdType.MESH
+        )
+
+    def greet(step, carry):
+        other = lax.rem(spot + step, near_group)
+        hello(device(position, other // near, side * near + lax.rem(other, near)))
+        return carry
+
+    hello(across)
+    hello(beside)
+    lax.fori_loop(1, near_group, greet, 0)
+
     @pl.when(position == 0)
     def _():
         pltpu.make_async_copy(stored, raw, load_sem).start()
 
-    barrier = pltpu.get_barrier_semaphore()
-    total = halves * groups
-    me = position * groups + member
-
-    def greet(step, carry):
-        other = lax.rem(me + step, total)
-        owner = lax.rem(other, groups)
-        pl.semaphore_signal(
-            barrier,
-            inc=1,
-            device_id=device(other // groups, owner // count_pz, lax.rem(owner, count_pz)),
-            device_id_type=pl.DeviceIdType.MESH,
-        )
-        return carry
-
-    lax.fori_loop(1, total, greet, 0)
+    loads = [
+        pltpu.make_async_copy(source, target, table_sem.at[i])
+        for i, (source, target) in enumerate(zip(kept_tables, loaded))
+    ]
+    for load in loads:
+        load.start()
+    for load in loads:
+        load.wait()
+    lanes = plane_refs[0]
+    turn, wave_z = lanes[0:1, :], lanes[1:2, :]
 
     def project(values, wave_y):
         wave_x = wave_x_ref[...]
@@ -492,7 +504,7 @@
 
         lax.fori_loop(0, rows, first, 0)
 
-    pl.semaphore_wait(barrier, total - 1)
+    pl.semaphore_wait(barrier, near_group + 1)
 
     def rebuild(slot, a, owner):
         wave_y = wave_y_of(a, owner)
@@ -572,54 +584,64 @@
 
             lax.fori_loop(1, near_group, push, 0)
 
-    @pl.when(position == 0)
-    def _():
-        each(band, rows, lambda a: own_copy(a).start())
-        each(0, band, lambda a: pair_copy(a).start())
-        each(0, band, lambda a: own_copy(a).start())
-
-    @pl.when(position == 1)
-    def _():
-        def relay(a):
-            own_copy(a).wait_recv()
-            pair_copy(a).start()
-
-        each(band, rows, relay)
-
-    transform(0, 0, 1, member, side)
+    def take_own(a):
+        own_copy(a).wait_recv()
+        pair_copy(a).start()
 
     def take_pair(a):
         pair_copy(a).wait_recv()
         relay_copy(a).start()
 
+    @pl.when(position == 0)
+    def _():
+        each(band + 1, rows, lambda a: own_copy(a).start())
+        own_copy(band).start()
+        own_copy(band - 1).start()
+        each(0, band - 1, lambda a: own_copy(a).start())
+        each(0, band // 2, lambda a: pair_copy(a).start())
+
     @pl.when(position == 1)
     def _():
+        each(band + 1, rows, take_own)
+        take_own(band)
+
+    transform(0, 0, 1, member, side)
+
+    @pl.when(position == 0)
+    def _():
+        each(band // 2, band, lambda a: pair_copy(a).start())
+
+    @pl.when(position == 1)
+    def _():
+        take_own(band - 1)
+
         def weave(a):
-            take_pair(a + band)
+            take_pair(a + band + 1)
             own_copy(a).wait_recv()
 
         each(0, band - 1, weave)
-        own_copy(band - 1).wait_recv()
 
     transform(1, 0, 0, member, side)
 
     @pl.when(position == 0)
     def _():
-        each(0, band, take_pair)
+        pair_copy(band).start()
+        each(0, band - 1, take_pair)
+        pair_copy(band - 1).wait_recv()
 
     @pl.when(position == 1)
     def _():
-        take_pair(rows - 1)
+        pair_copy(band).wait_recv()
 
     transform(2, 1, position, pair_member, 1 - side)
 
     @pl.when(position == 0)
     def _():
-        each(band, rows, lambda a: relay_copy(a).wait_recv())
+        each(band, rows, lambda a: pair_copy(a).wait_recv())
 
     @pl.when(position == 1)
     def _():
-        each(0, band, lambda a: relay_copy(a).wait_recv())
+        each(0, band, lambda a: pair_copy(a).wait_recv())
 
     transform(3, 1, 1 - position, pair_member, 1 - side)
 
@@ -634,6 +656,12 @@
 
     def plane_pair(k, carry):
         await_fields(3 + k, 5 * k, 5)
+
+        @pl.when(jnp.logical_and(position == 1, k == 0))
+        def _():
+            pl.semaphore_signal(
+                ready, inc=1, device_id=across, device_id_type=pl.DeviceIdType.MESH
+            )
 
         def plane(odd, carry):
             p = 2 * k + odd
@@ -647,6 +675,10 @@
             v0 = field(4, odd)
             for f, values in enumerate(plane_math([v0, v1, v2, d1, d2], tables)):
                 result[p, :, f] = values.reshape(groups, rows, retained)
+
+            @pl.when(jnp.logical_and(position == 0, p == 0))
+            def _():
+                pl.semaphore_wait(ready, 1)
 
             def push(turn_index, carry):
                 to_place = lax.rem(place + near + turn_index // count_py, count_pz)
@@ -704,20 +736,20 @@
         each(0, early, await_plane)
 
         def begin(a):
-            partial_sum[a] = dot3((fa0[...], fa1[...]), gather(0, early, a))
+            before = jnp.concatenate(rebuild(0, a, member), axis=1)
+            change = dot3((fa0[...], fa1[...]), gather(0, early, a))
+            partial_sum[a] = before + time_step * change
 
         each(0, rows, begin)
         each(early, planes, await_plane)
 
         def finish(a):
-            change = partial_sum[a] + dot3((fb0[...], fb1[...]), gather(early, planes - early, a))
-            wave_y = wave_y_of(a, member)
-            before = rebuild(0, a, member)
-            values = [
-                before[f] + time_step * change[:, f * retained : (f + 1) * retained]
-                for f in range(3)
-            ]
-            values, squared = project(values, wave_y)
+            change = dot3((fb0[...], fb1[...]), gather(early, planes - early, a))
+            after = partial_sum[a] + time_step * change
+            values, squared = project(
+                [after[:, f * retained : (f + 1) * retained] for f in range(3)],
+                wave_y_of(a, member),
+            )
             damping = jnp.exp((-viscosity * time_step) * squared)
             for f in range(3):
                 view, rows_of = strided(out, f, a)
@@ -753,10 +785,11 @@
     vmem = pl.BlockSpec(memory_space=pltpu.VMEM)
     return pl.pallas_call(
         step_kernel,
-        in_specs=[pl.BlockSpec(memory_space=pl.ANY)] + [vmem] * len(tables),
+        in_specs=[pl.BlockSpec(memory_space=pl.ANY)] * (1 + len(tables)),
         out_specs=vmem,
         out_shape=jax.ShapeDtypeStruct(stored.shape, jnp.float32),
-        scratch_shapes=[
+        scratch_shapes=[pltpu.VMEM(table.shape, table.dtype) for table in tables]
+        + [
             pltpu.VMEM(stored.shape, jnp.float32),
             pltpu.VMEM((2, rows, 2 * retained + 8, retained), jnp.float32),
             pltpu.VMEM((4, 5 * pairs, near_group, rows, retained), jnp.float32),
@@ -765,6 +798,7 @@
             pltpu.VMEM((planes, halves * groups, 3, rows, retained), jnp.float32),
             pltpu.VMEM((rows, retained, 3 * retained), jnp.float32),
             pltpu.SemaphoreType.DMA,
+            pltpu.SemaphoreType.DMA((len(tables),)),
             pltpu.SemaphoreType.DMA,
             pltpu.SemaphoreType.DMA((rows,)),
             pltpu.SemaphoreType.DMA((rows,)),
@@ -772,6 +806,7 @@
             pltpu.SemaphoreType.DMA((3 + pairs,)),
             pltpu.SemaphoreType.DMA,
             pltpu.SemaphoreType.DMA((planes,)),
+            pltpu.SemaphoreType.REGULAR,
         ],
         compiler_params=pltpu.CompilerParams(
             has_side_effects=True, collective_id=0, vmem_limit_bytes=56 * 1024 * 1024

time: 94 us -> 87.3 us (0.929)
  Pallas kernels: 89.2 us -> 83.4 us
    pallas_call x1, Pallas kernels: 89.2 us -> 83.4 us  [helped_advance(): pl.pallas_call(step_kernel, in_specs=[pl.BlockSpec(memory_space=pl.ANY)]...]
where the time goes in v2:
time: 87.3 us; the launch traced here: 87 us
  Pallas kernels  83.4 us (96%)
  local copies, waits for them, and re-layouts  3.63 us (4%)
    pallas_call x1, Pallas kernels, helped_advance(): pl.pallas_call(step_kernel, in_specs=[pl.BlockSpec(memory_space=pl.ANY)]...  83.4 us
    unnamed x1, local copies, waits for them, and re-layouts  3.63 us

profile of v2, /device:TPU:3, one launch (start us, length us, event | category | flops | bytes accessed | tf_op | source)
XLA Modules:
  0.0 87.0 jit_solution(18106635069518378739)
XLA Ops:
  0.0 83.4 %step.1 = f32[3,128,8,128]{3,2,1,0:T(8,128)} custom-call(f32[3,128,8,128]{3,2,1,0:T(8,128)} %bitcast.5, f32[128,128]{1,0:T(8,128)} %constant.34.clone.refs_1_, bf16[4,96,256]{2,1,0:T(8,128)(2,1)} %constant.35.clone.refs_2_, bf16[4,96,256]{2,1,0:T(8,128)(2,1)} %constant.36.clone.refs_3_, bf16[128,256]{1,0:T(8,128)(2,1)} %constant.37.clone.refs_4_, ...), custom_call_target="tpu_custom_call" | custom-call | tf_op jit(solution)/shard_map/step/pallas_call | solution.py:786
  83.4 3.6 %copy.21 = f32[1,3,128,8,1,128]{5,4,3,2,1,0:T(1,128)} copy(f32[1,3,128,8,1,128]{5,4,3,2,1,0:T(1,128)} %bitcast.4) | data formatting | bytes 3145728

commit v3 on v2

--- a/solution.py
+++ b/solution.py
@@ -787,7 +787,7 @@
         step_kernel,
         in_specs=[pl.BlockSpec(memory_space=pl.ANY)] * (1 + len(tables)),
         out_specs=vmem,
-        out_shape=jax.ShapeDtypeStruct(stored.shape, jnp.float32),
+        out_shape=pltpu.VMEM(stored.shape, jnp.float32),
         scratch_shapes=[pltpu.VMEM(table.shape, table.dtype) for table in tables]
         + [
             pltpu.VMEM(stored.shape, jnp.float32),

time: 87.3 us -> 83.6 us (0.958)
  local copies, waits for them, and re-layouts: 3.63 us -> 1.15 us
  Pallas kernels: 83.4 us -> 82.2 us
    unnamed x1, local copies, waits for them, and re-layouts: 3.63 us -> 1.15 us
    pallas_call x1, Pallas kernels: 83.4 us -> 82.2 us  [helped_advance(): pl.pallas_call(step_kernel, in_specs=[pl.BlockSpec(memory_space=pl.ANY)]...]
where the time goes in v3:
time: 83.6 us; the launch traced here: 83.4 us
  Pallas kernels  82.2 us (98%)
  local copies, waits for them, and re-layouts  1.15 us (1%)
    pallas_call x1, Pallas kernels, helped_advance(): pl.pallas_call(step_kernel, in_specs=[pl.BlockSpec(memory_space=pl.ANY)]...  82.2 us

profile of v3, /device:TPU:3, one launch (start us, length us, event | category | flops | bytes accessed | tf_op | source)
XLA Modules:
  0.0 83.4 jit_solution(859196334104104682)
XLA Ops:
  0.0 82.2 %step.1 = f32[3,128,8,128]{3,2,1,0:T(8,128)S(1)} custom-call(f32[3,128,8,128]{3,2,1,0:T(8,128)} %bitcast.5, f32[128,128]{1,0:T(8,128)} %constant.34.clone.refs_1_, bf16[4,96,256]{2,1,0:T(8,128)(2,1)} %constant.35.clone.refs_2_, bf16[4,96,256]{2,1,0:T(8,128)(2,1)} %constant.36.clone.refs_3_, bf16[128,256]{1,0:T(8,128)(2,1)} %constant.37.clone.refs_4_, ...), custom_call_target="tpu_custom_call" | custom-call | tf_op jit(solution)/shard_map/step/pallas_call | solution.py:786
  82.2 1.1 %copy.21 = f32[1,3,128,8,1,128]{5,4,3,2,1,0:T(1,128)} copy(f32[1,3,128,8,1,128]{5,4,3,2,1,0:T(1,128)S(1)} %bitcast.4) | data formatting | bytes 3145728

commit v4 on v3

--- a/solution.py
+++ b/solution.py
@@ -267,16 +267,17 @@
 def wave_order(retained, count_py, count_pz):
     groups = count_py * count_pz
     rows, near = retained // groups, count_pz // 2
-    side, band, line, z_low, inner = np.meshgrid(
+    half, side, high, line, z_low, inner = np.meshgrid(
+        np.arange(2),
         np.arange(2),
         np.arange(2),
         np.arange(count_py),
         np.arange(near),
-        np.arange(rows // 2),
+        np.arange(rows // 4),
         indexing="ij",
     )
     owner = line * count_pz + side * near + z_low
-    return ((band * (rows // 2) + inner) * groups + owner).reshape(-1)
+    return (((high * 2 + half) * (rows // 4) + inner) * groups + owner).reshape(-1)
 
 
 def plane_tables(extent, retained, count_py, count_pz):
@@ -385,9 +386,10 @@
     loaded = refs[19:36]
     wave_x_ref, xi0, xi1, fa0, fa1, fb0, fb1 = loaded[:7]
     plane_refs = loaded[7:]
-    raw, modes, spread, recv, result, arrived, partial_sum = refs[36:43]
-    load_sem, table_sem, mode_send, own_recv, pair_recv = refs[43:48]
-    field_send, field_recv, back_send, back_recv, ready = refs[48:]
+    raw, modes, spread, spread_mean, recv, recv_mean = refs[36:42]
+    result, arrived, partial_sum = refs[42:45]
+    load_sem, table_sem, mode_send, own_recv, pair_recv = refs[45:50]
+    field_send, field_recv, mean_recv, back_send, back_recv, ready = refs[50:]
 
     _, retained, rows, _ = stored.shape
     planes, groups = result.shape[:2]
@@ -535,13 +537,19 @@
 
         lax.fori_loop(start, stop, body, 0)
 
-    def transform(step, slot, high, owner, slot_side):
+    few = band // 2
+    last = 7
+
+    def transform(step, slot, high, half):
+        owner = pair_member if slot else member
         quadrant = position * 2 + side
         tables = (xi0[quadrant], xi1[quadrant])
-        fields = [rebuild(slot, high * band + a, owner) for a in range(band)]
+        top_row = high * band + half * few
+        fields = [rebuild(slot, top_row + a, owner) for a in range(few)]
         points = planes * near_group
+        chunk = (1 - side if slot else side) * 2 + high
         for f in (1, 2, 0):
-            parts = [fields[a][f] for a in range(band)]
+            parts = [fields[a][f] for a in range(few)]
             stacked = jnp.concatenate(
                 [
                     jnp.concatenate(parts, axis=1),
@@ -554,108 +562,125 @@
             for p in range(planes):
                 for c in range(count):
                     if f:
-                        group, offset = p // 2 * 5 + p % 2 * 2 + f - 1, c
+                        view, offset = spread.at[step, p], 2 * (f - 1) + c
                     else:
-                        group, offset = p // 2 * 5 + 4, p % 2
-                    view = spread.at[step, group].reshape(near_group * rows, retained)
+                        view, offset = spread_mean.at[step // 2, p // 2], 2 * half + p % 2
+                    view = view.reshape(near_group * rows, retained)
                     top = c * points + p * near_group
-                    for a in range(band):
-                        view[pl.ds(2 * a + offset, near_group, stride=rows), :] = moved[
+                    for a in range(few):
+                        view[pl.ds(4 * a + offset, near_group, stride=rows), :] = moved[
                             top : top + near_group, a * retained : (a + 1) * retained
                         ]
-        chunk = slot_side * 2 + high
-        slots = chunk * near_group
+        slots = (half * 4 + chunk) * near_group
+        mean_slots = chunk * near_group
+        complete = step % 2 == 1
         recv[:, slots + spot] = spread[step, :, spot]
-        spans = [(step, 0, 5 * pairs)]
-        if step == 3:
-            spans = [(step + k, 5 * k, 5) for k in range(pairs)]
-        for semaphore, start, count in spans:
-
-            def push(turn_index, carry, semaphore=semaphore, start=start, count=count):
-                other = lax.rem(spot + near_group - turn_index, near_group)
+        if complete:
+            recv_mean[:, mean_slots + spot] = spread_mean[step // 2, :, spot]
+
+        def send(other, first, count, index, mean_index):
+            to = device(position, other // near, side * near + lax.rem(other, near))
+            remote(
+                spread.at[step, pl.ds(2 * first, 2 * count), other],
+                recv.at[pl.ds(2 * first, 2 * count), slots + spot],
+                field_send,
+                field_recv.at[index],
+                to,
+            ).start()
+            if complete:
                 remote(
-                    spread.at[step, pl.ds(start, count), other],
-                    recv.at[pl.ds(start, count), slots + spot],
+                    spread_mean.at[step // 2, pl.ds(first, count), other],
+                    recv_mean.at[pl.ds(first, count), mean_slots + spot],
                     field_send,
-                    field_recv.at[semaphore],
-                    device(position, other // near, side * near + lax.rem(other, near)),
+                    mean_recv.at[mean_index],
+                    to,
                 ).start()
+
+        spans = [(0, pairs, step, step // 2)]
+        if step == last:
+            spans = [(k, 1, last + k, last // 2 + k) for k in range(pairs)]
+        for first, count, index, mean_index in spans:
+
+            def push(turn_index, carry, span=(first, count, index, mean_index)):
+                send(lax.rem(spot + near_group - turn_index, near_group), *span)
                 return carry
 
             lax.fori_loop(1, near_group, push, 0)
 
-    def take_own(a):
-        own_copy(a).wait_recv()
-        pair_copy(a).start()
-
-    def take_pair(a):
-        pair_copy(a).wait_recv()
-        relay_copy(a).start()
-
-    @pl.when(position == 0)
-    def _():
-        each(band + 1, rows, lambda a: own_copy(a).start())
-        own_copy(band).start()
-        own_copy(band - 1).start()
-        each(0, band - 1, lambda a: own_copy(a).start())
-        each(0, band // 2, lambda a: pair_copy(a).start())
-
-    @pl.when(position == 1)
-    def _():
-        each(band + 1, rows, take_own)
-        take_own(band)
-
-    transform(0, 0, 1, member, side)
-
-    @pl.when(position == 0)
-    def _():
-        each(band // 2, band, lambda a: pair_copy(a).start())
-
-    @pl.when(position == 1)
-    def _():
-        take_own(band - 1)
-
-        def weave(a):
-            take_pair(a + band + 1)
+    def await_fields(first, count, index):
+        some = recv.at[pl.ds(2 * first, 2 * count), pl.ds(0, near_group - 1)]
+        remote(some, some, field_send, field_recv.at[index], beside).wait_recv()
+
+    def await_means(first, count, index):
+        some = recv_mean.at[pl.ds(first, count), pl.ds(0, near_group - 1)]
+        remote(some, some, field_send, mean_recv.at[index], beside).wait_recv()
+
+    low, high = list(range(band)), list(range(band, rows))
+    own_order = high + low[::-1]
+
+    def send_pair(rows_of):
+        for a in rows_of:
+            pair_copy(a).start()
+
+    def take_own(rows_of):
+        for a in rows_of:
             own_copy(a).wait_recv()
-
-        each(0, band - 1, weave)
-
-    transform(1, 0, 0, member, side)
-
-    @pl.when(position == 0)
-    def _():
-        pair_copy(band).start()
-        each(0, band - 1, take_pair)
-        pair_copy(band - 1).wait_recv()
-
-    @pl.when(position == 1)
-    def _():
-        pair_copy(band).wait_recv()
-
-    transform(2, 1, position, pair_member, 1 - side)
-
-    @pl.when(position == 0)
-    def _():
-        each(band, rows, lambda a: pair_copy(a).wait_recv())
-
-    @pl.when(position == 1)
-    def _():
-        each(0, band, lambda a: pair_copy(a).wait_recv())
-
-    transform(3, 1, 1 - position, pair_member, 1 - side)
-
-    def await_fields(semaphore, start, count):
-        some = recv.at[pl.ds(start, count), pl.ds(0, near_group - 1)]
-        remote(some, some, field_send, field_recv.at[semaphore], beside).wait_recv()
-
-    for step in range(3):
-        await_fields(step, 0, 5 * pairs)
+            if a in high:
+                pair_copy(a).start()
+
+    def take_pair(rows_of):
+        for a in rows_of:
+            pair_copy(a).wait_recv()
+
+            @pl.when(position == (0 if a in low else 1))
+            def _():
+                relay_copy(a).start()
+
+    def on(which, do):
+        @pl.when(position == which)
+        def _():
+            do()
+
+    def start_first():
+        for a in own_order:
+            own_copy(a).start()
+        send_pair(low[:2])
+
+    on(0, start_first)
+    on(1, lambda: take_own(high[:few]))
+    transform(0, 0, 1, 0)
+    on(0, lambda: send_pair(low[2:3]))
+    on(1, lambda: take_own(high[few:]))
+    transform(1, 0, 1, 1)
+    on(0, lambda: send_pair(low[3:]))
+    on(1, lambda: take_own(low[few:][::-1]))
+    on(1, lambda: take_pair(high[:1]))
+    transform(2, 0, 0, 1)
+    on(1, lambda: take_own(low[:few][::-1]))
+    transform(3, 0, 0, 0)
+    on(0, lambda: take_pair(low[:few]))
+    on(1, lambda: take_pair(high[1:few]))
+    transform(4, 1, position, 0)
+    on(0, lambda: take_pair(low[few:]))
+    on(1, lambda: take_pair(high[few:]))
+    transform(5, 1, position, 1)
+    on(0, lambda: take_pair(high[:few]))
+    on(1, lambda: take_pair(low[:few]))
+    transform(6, 1, 1 - position, 0)
+    on(0, lambda: take_pair(high[few:]))
+    on(1, lambda: take_pair(low[few:]))
+    transform(7, 1, 1 - position, 1)
+
+    for step in range(last):
+        await_fields(0, pairs, step)
+    for step in range(last // 2):
+        await_means(0, pairs, step)
 
     tables = [ref[...] for ref in plane_refs]
 
     def plane_pair(k, carry):
-        await_fields(3 + k, 5 * k, 5)
+        await_fields(k, 1, last + k)
+        await_means(k, 1, last // 2 + k)
 
         @pl.when(jnp.logical_and(position == 1, k == 0))
         def _():
@@ -666,13 +691,16 @@
         def plane(odd, carry):
             p = 2 * k + odd
 
-            def field(group, offset):
-                view = recv.at[5 * k + group].reshape(4 * near_group * rows, retained)
-                return view[pl.ds(offset, retained, stride=2), :]
-
-            v1, d1 = field(2 * odd, 0), field(2 * odd, 1)
-            v2, d2 = field(2 * odd + 1, 0), field(2 * odd + 1, 1)
-            v0 = field(4, odd)
+            view = recv.at[p].reshape(8 * near_group * rows, retained)
+            v1, d1, v2, d2 = [view[pl.ds(i, retained, stride=4), :] for i in range(4)]
+            view = recv_mean.at[k].reshape(4 * near_group * rows, retained)
+            v0 = jnp.concatenate(
+                [
+                    view[pl.ds(2 * half + odd, retained // 2, stride=4), :]
+                    for half in range(2)
+                ],
+                axis=0,
+            )
             for f, values in enumerate(plane_math([v0, v1, v2, d1, d2], tables)):
                 result[p, :, f] = values.reshape(groups, rows, retained)
 
@@ -757,8 +785,9 @@
 
         each(0, rows, finish)
 
-    some = spread.at[:, :, pl.ds(0, near_group - 1)]
-    remote(some, some, field_send, field_recv.at[0], beside).wait_send()
+    for sent in (spread, spread_mean):
+        some = sent.at[:, :, pl.ds(0, near_group - 1)]
+        remote(some, some, field_send, field_recv.at[0], beside).wait_send()
 
     @pl.when(position == 0)
     def _():
@@ -792,8 +821,10 @@
         + [
             pltpu.VMEM(stored.shape, jnp.float32),
             pltpu.VMEM((2, rows, 2 * retained + 8, retained), jnp.float32),
-            pltpu.VMEM((4, 5 * pairs, near_group, rows, retained), jnp.float32),
-            pltpu.VMEM((5 * pairs, 4 * near_group, rows, retained), jnp.float32),
+            pltpu.VMEM((8, planes, near_group, rows, retained), jnp.float32),
+            pltpu.VMEM((4, pairs, near_group, rows, retained), jnp.float32),
+            pltpu.VMEM((planes, 8 * near_group, rows, retained), jnp.float32),
+            pltpu.VMEM((pairs, 4 * near_group, rows, retained), jnp.float32),
             pltpu.VMEM((planes, groups, 3, rows, retained), jnp.float32),
             pltpu.VMEM((planes, halves * groups, 3, rows, retained), jnp.float32),
             pltpu.VMEM((rows, retained, 3 * retained), jnp.float32),
@@ -803,6 +834,7 @@
             pltpu.SemaphoreType.DMA((rows,)),
             pltpu.SemaphoreType.DMA((rows,)),
             pltpu.SemaphoreType.DMA,
+            pltpu.SemaphoreType.DMA((7 + pairs,)),
             pltpu.SemaphoreType.DMA((3 + pairs,)),
             pltpu.SemaphoreType.DMA,
             pltpu.SemaphoreType.DMA((planes,)),

time: 83.6 us -> 79.6 us (0.952)
  Pallas kernels: 82.2 us -> 78.3 us
    pallas_call x1, Pallas kernels: 82.2 us -> 78.3 us  [helped_advance(): pl.pallas_call(step_kernel, in_specs=[pl.BlockSpec(memory_space=pl.ANY)]...]
where the time goes in v4:
time: 79.6 us; the launch traced here: 79.4 us
  Pallas kernels  78.3 us (98%)
  local copies, waits for them, and re-layouts  1.15 us (1%)
    pallas_call x1, Pallas kernels, helped_advance(): pl.pallas_call(step_kernel, in_specs=[pl.BlockSpec(memory_space=pl.ANY)]...  78.3 us

profile of v4, /device:TPU:3, one launch (start us, length us, event | category | flops | bytes accessed | tf_op | source)
XLA Modules:
  0.0 79.4 jit_solution(7698539932963499407)
XLA Ops:
  0.0 78.3 %step.1 = f32[3,128,8,128]{3,2,1,0:T(8,128)S(1)} custom-call(f32[3,128,8,128]{3,2,1,0:T(8,128)} %bitcast.5, f32[128,128]{1,0:T(8,128)} %constant.34.clone.refs_1_, bf16[4,96,256]{2,1,0:T(8,128)(2,1)} %constant.35.clone.refs_2_, bf16[4,96,256]{2,1,0:T(8,128)(2,1)} %constant.36.clone.refs_3_, bf16[128,256]{1,0:T(8,128)(2,1)} %constant.37.clone.refs_4_, ...), custom_call_target="tpu_custom_call" | custom-call | tf_op jit(solution)/shard_map/step/pallas_call | solution.py:815
  78.3 1.1 %copy.21 = f32[1,3,128,8,1,128]{5,4,3,2,1,0:T(1,128)} copy(f32[1,3,128,8,1,128]{5,4,3,2,1,0:T(1,128)S(1)} %bitcast.4) | data formatting | bytes 3145728

commit v5 on v4

--- a/solution.py
+++ b/solution.py
@@ -387,9 +387,9 @@
     wave_x_ref, xi0, xi1, fa0, fa1, fb0, fb1 = loaded[:7]
     plane_refs = loaded[7:]
     raw, modes, spread, spread_mean, recv, recv_mean = refs[36:42]
-    result, arrived, partial_sum = refs[42:45]
-    load_sem, table_sem, mode_send, own_recv, pair_recv = refs[45:50]
-    field_send, field_recv, mean_recv, back_send, back_recv, ready = refs[50:]
+    result, arrived, partial_sum, scales = refs[42:46]
+    load_sem, table_sem, mode_send, own_recv, pair_recv = refs[46:51]
+    field_send, field_recv, mean_recv, back_send, back_recv = refs[51:]
 
     _, retained, rows, _ = stored.shape
     planes, groups = result.shape[:2]
@@ -444,7 +444,8 @@
 
     def greet(step, carry):
         other = lax.rem(spot + step, near_group)
-        hello(device(position, other // near, side * near + lax.rem(other, near)))
+        for half in range(halves):
+            hello(device(half, other // near, side * near + lax.rem(other, near)))
         return carry
 
     hello(across)
@@ -459,10 +460,11 @@
         pltpu.make_async_copy(source, target, table_sem.at[i])
         for i, (source, target) in enumerate(zip(kept_tables, loaded))
     ]
-    for load in loads:
-        load.start()
-    for load in loads:
-        load.wait()
+    needed = (0, 7)
+    for i in needed:
+        loads[i].start()
+    for i in needed:
+        loads[i].wait()
     lanes = plane_refs[0]
     turn, wave_z = lanes[0:1, :], lanes[1:2, :]
 
@@ -477,7 +479,7 @@
             values[1] - wave_y * divergence,
             values[2] - wave_z * divergence,
         ]
-        return projected, squared
+        return projected
 
     def flat_squares(wave_y):
         squares = wave_y * wave_y + wave_z * wave_z
@@ -487,13 +489,18 @@
     def _():
         pltpu.make_async_copy(stored, raw, load_sem).wait()
 
+    for i, load in enumerate(loads):
+        if i not in needed:
+            load.start()
+
+    def enter(start, stop):
         def first(a, carry):
             wave_y = wave_y_of(a, member)
             values = []
             for f in range(3):
                 view, rows_of = strided(raw, f, a)
                 values.append(view[rows_of, :])
-            values, _ = project(values, wave_y)
+            values = project(values, wave_y)
             for f in range(3):
                 view, rows_of = strided(out, f, a)
                 view[rows_of, :] = values[f]
@@ -504,9 +511,13 @@
             modes[0, a, 2 * retained : 2 * retained + 8, :] = values[0][0:8]
             return carry
 
-        lax.fori_loop(0, rows, first, 0)
-
-    pl.semaphore_wait(barrier, near_group + 1)
+        lax.fori_loop(start, stop, first, 0)
+
+    @pl.when(position == 0)
+    def _():
+        enter(band, rows)
+
+    pl.semaphore_wait(barrier, 2 * near_group)
 
     def rebuild(slot, a, owner):
         wave_y = wave_y_of(a, owner)
@@ -538,16 +549,20 @@
         lax.fori_loop(start, stop, body, 0)
 
     few = band // 2
-    last = 7
+    final = 5
+    crossing = 6
+    late = 8
 
     def transform(step, slot, high, half):
         owner = pair_member if slot else member
-        quadrant = position * 2 + side
-        tables = (xi0[quadrant], xi1[quadrant])
         top_row = high * band + half * few
         fields = [rebuild(slot, top_row + a, owner) for a in range(few)]
         points = planes * near_group
         chunk = (1 - side if slot else side) * 2 + high
+        slots = (half * 4 + chunk) * near_group
+        mean_slots = chunk * near_group
+        complete = step % 2 == 1
+        operands = []
         for f in (1, 2, 0):
             parts = [fields[a][f] for a in range(few)]
             stacked = jnp.concatenate(
@@ -557,62 +572,82 @@
                 ],
                 axis=0,
             )
-            count = 2 if f else 1
-            moved = dot3([t[: count * points] for t in tables], split(stacked))
-            for p in range(planes):
-                for c in range(count):
-                    if f:
-                        view, offset = spread.at[step, p], 2 * (f - 1) + c
-                    else:
-                        view, offset = spread_mean.at[step // 2, p // 2], 2 * half + p % 2
-                    view = view.reshape(near_group * rows, retained)
-                    top = c * points + p * near_group
-                    for a in range(few):
-                        view[pl.ds(4 * a + offset, near_group, stride=rows), :] = moved[
-                            top : top + near_group, a * retained : (a + 1) * retained
-                        ]
-        slots = (half * 4 + chunk) * near_group
-        mean_slots = chunk * near_group
-        complete = step % 2 == 1
-        recv[:, slots + spot] = spread[step, :, spot]
-        if complete:
-            recv_mean[:, mean_slots + spot] = spread_mean[step // 2, :, spot]
-
-        def send(other, first, count, index, mean_index):
-            to = device(position, other // near, side * near + lax.rem(other, near))
-            remote(
-                spread.at[step, pl.ds(2 * first, 2 * count), other],
-                recv.at[pl.ds(2 * first, 2 * count), slots + spot],
-                field_send,
-                field_recv.at[index],
-                to,
-            ).start()
-            if complete:
+            operands.append((f, split(stacked)))
+
+        def deliver(target, place_in, away):
+            tables = (xi0[target * 2 + side], xi1[target * 2 + side])
+            for f, stacked in operands:
+                count = 2 if f else 1
+                moved = dot3([t[: count * points] for t in tables], stacked)
+                for p in range(planes):
+                    for c in range(count):
+                        if f:
+                            view, offset = spread.at[place_in, p], 2 * (f - 1) + c
+                        else:
+                            view, offset = spread_mean.at[place_in // 2, p // 2], 2 * half + p % 2
+                        view = view.reshape(near_group * rows, retained)
+                        top = c * points + p * near_group
+                        for a in range(few):
+                            view[pl.ds(4 * a + offset, near_group, stride=rows), :] = moved[
+                                top : top + near_group, a * retained : (a + 1) * retained
+                            ]
+            if not away:
+                recv[:, slots + spot] = spread[place_in, :, spot]
+                if complete:
+                    recv_mean[:, mean_slots + spot] = spread_mean[place_in // 2, :, spot]
+
+            def send(other, first, count, index, mean_index):
+                to = device(target, other // near, side * near + lax.rem(other, near))
                 remote(
-                    spread_mean.at[step // 2, pl.ds(first, count), other],
-                    recv_mean.at[pl.ds(first, count), mean_slots + spot],
+                    spread.at[place_in, pl.ds(2 * first, 2 * count), other],
+                    recv.at[pl.ds(2 * first, 2 * count), slots + spot],
                     field_send,
-                    mean_recv.at[mean_index],
+                    field_recv.at[index],
                     to,
                 ).start()
-
-        spans = [(0, pairs, step, step // 2)]
-        if step == last:
-            spans = [(k, 1, last + k, last // 2 + k) for k in range(pairs)]
-        for first, count, index, mean_index in spans:
-
-            def push(turn_index, carry, span=(first, count, index, mean_index)):
-                send(lax.rem(spot + near_group - turn_index, near_group), *span)
-                return carry
-
-            lax.fori_loop(1, near_group, push, 0)
-
-    def await_fields(first, count, index):
-        some = recv.at[pl.ds(2 * first, 2 * count), pl.ds(0, near_group - 1)]
+                if complete:
+                    remote(
+                        spread_mean.at[place_in // 2, pl.ds(first, count), other],
+                        recv_mean.at[pl.ds(first, count), mean_slots + spot],
+                        field_send,
+                        mean_recv.at[mean_index],
+                        to,
+                    ).start()
+
+            index, mean_index = field_index(place_in), mean_index_of(place_in)
+            spans = [(0, pairs, index, mean_index)]
+            if step in (final, late + 1):
+                spans = [(k, 1, index + k, mean_index + k) for k in range(pairs)]
+            for span in spans:
+
+                def push(turn_index, carry, span=span, send=send):
+                    send(lax.rem(spot + near_group - turn_index, near_group), *span)
+                    return carry
+
+                lax.fori_loop(0 if away else 1, near_group, push, 0)
+
+        if step in (final - 1, final):
+
+            @pl.when(position == 0)
+            def _():
+                deliver(1, step + 2, True)
+
+        deliver(position, step, False)
+
+    def field_index(place_in):
+        if place_in >= late:
+            place_in -= 2
+        return place_in if place_in <= final else place_in - 1 + pairs
+
+    def mean_index_of(place_in):
+        return place_in // 2 if place_in <= final else final // 2 + pairs
+
+    def await_fields(first, count, index, senders):
+        some = recv.at[pl.ds(2 * first, 2 * count), pl.ds(0, senders)]
         remote(some, some, field_send, field_recv.at[index], beside).wait_recv()
 
-    def await_means(first, count, index):
-        some = recv_mean.at[pl.ds(first, count), pl.ds(0, near_group - 1)]
+    def await_means(first, count, index, senders):
+        some = recv_mean.at[pl.ds(first, count), pl.ds(0, senders)]
         remote(some, some, field_send, mean_recv.at[index], beside).wait_recv()
 
     low, high = list(range(band)), list(range(band, rows))
@@ -631,10 +666,11 @@
     def take_pair(rows_of):
         for a in rows_of:
             pair_copy(a).wait_recv()
-
-            @pl.when(position == (0 if a in low else 1))
-            def _():
-                relay_copy(a).start()
+            if a in high:
+
+                @pl.when(position == 1)
+                def _():
+                    relay_copy(a).start()
 
     def on(which, do):
         @pl.when(position == which)
@@ -642,11 +678,17 @@
             do()
 
     def start_first():
-        for a in own_order:
+        for a in high:
             own_copy(a).start()
+        enter(0, band)
         send_pair(low[:2])
+        for a in low[::-1]:
+            own_copy(a).start()
 
     on(0, start_first)
+    for i, load in enumerate(loads):
+        if i not in needed:
+            load.wait()
     on(1, lambda: take_own(high[:few]))
     transform(0, 0, 1, 0)
     on(0, lambda: send_pair(low[2:3]))
@@ -664,29 +706,34 @@
     on(0, lambda: take_pair(low[few:]))
     on(1, lambda: take_pair(high[few:]))
     transform(5, 1, position, 1)
-    on(0, lambda: take_pair(high[:few]))
-    on(1, lambda: take_pair(low[:few]))
-    transform(6, 1, 1 - position, 0)
-    on(0, lambda: take_pair(high[few:]))
-    on(1, lambda: take_pair(low[few:]))
-    transform(7, 1, 1 - position, 1)
-
-    for step in range(last):
-        await_fields(0, pairs, step)
-    for step in range(last // 2):
-        await_means(0, pairs, step)
+
+    def finish_late():
+        take_pair(high[:few])
+        transform(late, 1, 1, 0)
+        take_pair(high[few:])
+        transform(late + 1, 1, 1, 1)
+
+    on(0, finish_late)
+
+    for step in range(final):
+        await_fields(0, pairs, step, near_group - 1)
+    for step in range(final // 2):
+        await_means(0, pairs, step, near_group - 1)
+    on(0, lambda: await_fields(0, pairs, field_index(crossing), near_group - 1))
+    on(1, lambda: await_fields(0, pairs, field_index(crossing), near_group))
 
     tables = [ref[...] for ref in plane_refs]
 
     def plane_pair(k, carry):
-        await_fields(k, 1, last + k)
-        await_means(k, 1, last // 2 + k)
-
-        @pl.when(jnp.logical_and(position == 1, k == 0))
-        def _():
-            pl.semaphore_signal(
-                ready, inc=1, device_id=across, device_id_type=pl.DeviceIdType.MESH
-            )
+        await_fields(k, 1, final + k, near_group - 1)
+        await_means(k, 1, final // 2 + k, near_group - 1)
+
+        def await_last(senders):
+            await_fields(k, 1, field_index(crossing + 1) + k, senders)
+            await_means(k, 1, mean_index_of(crossing) + k, senders)
+
+        on(0, lambda: await_last(near_group - 1))
+        on(1, lambda: await_last(near_group))
 
         def plane(odd, carry):
             p = 2 * k + odd
@@ -703,10 +750,6 @@
             )
             for f, values in enumerate(plane_math([v0, v1, v2, d1, d2], tables)):
                 result[p, :, f] = values.reshape(groups, rows, retained)
-
-            @pl.when(jnp.logical_and(position == 0, p == 0))
-            def _():
-                pl.semaphore_wait(ready, 1)
 
             def push(turn_index, carry):
                 to_place = lax.rem(place + near + turn_index // count_py, count_pz)
@@ -767,36 +810,60 @@
             before = jnp.concatenate(rebuild(0, a, member), axis=1)
             change = dot3((fa0[...], fa1[...]), gather(0, early, a))
             partial_sum[a] = before + time_step * change
+            wave_x, wave_y = wave_x_ref[...], wave_y_of(a, member)
+            squared = wave_x * wave_x + (wave_y * wave_y + wave_z * wave_z)
+            damping = jnp.exp((-viscosity * time_step) * squared)
+            scales[0, a] = damping
+            scales[1, a] = damping / jnp.maximum(squared, 1.0)
 
         each(0, rows, begin)
         each(early, planes, await_plane)
 
-        def finish(a):
-            change = dot3((fb0[...], fb1[...]), gather(early, planes - early, a))
-            after = partial_sum[a] + time_step * change
-            values, squared = project(
-                [after[:, f * retained : (f + 1) * retained] for f in range(3)],
-                wave_y_of(a, member),
-            )
-            damping = jnp.exp((-viscosity * time_step) * squared)
-            for f in range(3):
-                view, rows_of = strided(out, f, a)
-                view[rows_of, :] = damping * values[f]
-
-        each(0, rows, finish)
-
-    for sent in (spread, spread_mean):
-        some = sent.at[:, :, pl.ds(0, near_group - 1)]
-        remote(some, some, field_send, field_recv.at[0], beside).wait_send()
+        def finish(pair):
+            sides = [gather(early, planes - early, 2 * pair + i) for i in range(2)]
+            both = [jnp.concatenate(parts, axis=1) for parts in zip(*sides)]
+            change = dot3((fb0[...], fb1[...]), both)
+            for i in range(2):
+                a = 2 * pair + i
+                after = partial_sum[a] + time_step * change[:, 3 * i * retained : 3 * (i + 1) * retained]
+                values = [after[:, f * retained : (f + 1) * retained] for f in range(3)]
+                waves = (wave_x_ref[...], wave_y_of(a, member), wave_z)
+                inner = sum(wave * value for wave, value in zip(waves, values)) * scales[1, a]
+                for f in range(3):
+                    view, rows_of = strided(out, f, a)
+                    view[rows_of, :] = scales[0, a] * values[f] - waves[f] * inner
+
+        each(0, rows // 2, finish)
+
+    def await_sends(*sent):
+        for some in sent:
+            remote(some, some, field_send, field_recv.at[0], beside).wait_send()
+
+    others = pl.ds(0, near_group - 1)
+    await_sends(
+        spread.at[pl.ds(0, crossing), :, others],
+        spread_mean.at[pl.ds(0, crossing // 2), :, others],
+    )
 
     @pl.when(position == 0)
     def _():
-        remote(modes, modes, mode_send, own_recv.at[0], beside).wait_send()
+        await_sends(
+            spread.at[pl.ds(crossing, 2)],
+            spread_mean.at[crossing // 2],
+            spread.at[pl.ds(late, 2), :, others],
+            spread_mean.at[late // 2, :, others],
+        )
+
+    some = modes.at[1, pl.ds(0, band)]
+    remote(modes.at[0], modes.at[0], mode_send, own_recv.at[0], beside).wait_send()
+
+    @pl.when(position == 0)
+    def _():
+        remote(some, some, mode_send, own_recv.at[0], beside).wait_send()
         remote(result, result, back_send, back_recv.at[0], beside).wait_send()
 
     @pl.when(position == 1)
     def _():
-        remote(modes.at[0], modes.at[0], mode_send, own_recv.at[0], beside).wait_send()
         some = result.at[:, pl.ds(0, groups - 1)]
         remote(some, some, back_send, back_recv.at[0], beside).wait_send()
 
@@ -821,24 +888,24 @@
         + [
             pltpu.VMEM(stored.shape, jnp.float32),
             pltpu.VMEM((2, rows, 2 * retained + 8, retained), jnp.float32),
-            pltpu.VMEM((8, planes, near_group, rows, retained), jnp.float32),
-            pltpu.VMEM((4, pairs, near_group, rows, retained), jnp.float32),
+            pltpu.VMEM((10, planes, near_group, rows, retained), jnp.float32),
+            pltpu.VMEM((5, pairs, near_group, rows, retained), jnp.float32),
             pltpu.VMEM((planes, 8 * near_group, rows, retained), jnp.float32),
             pltpu.VMEM((pairs, 4 * near_group, rows, retained), jnp.float32),
             pltpu.VMEM((planes, groups, 3, rows, retained), jnp.float32),
             pltpu.VMEM((planes, halves * groups, 3, rows, retained), jnp.float32),
             pltpu.VMEM((rows, retained, 3 * retained), jnp.float32),
+            pltpu.VMEM((2, rows, retained, retained), jnp.float32),
             pltpu.SemaphoreType.DMA,
             pltpu.SemaphoreType.DMA((len(tables),)),
             pltpu.SemaphoreType.DMA,
             pltpu.SemaphoreType.DMA((rows,)),
             pltpu.SemaphoreType.DMA((rows,)),
             pltpu.SemaphoreType.DMA,
-            pltpu.SemaphoreType.DMA((7 + pairs,)),
-            pltpu.SemaphoreType.DMA((3 + pairs,)),
+            pltpu.SemaphoreType.DMA((6 + 2 * pairs,)),
+            pltpu.SemaphoreType.DMA((2 + 2 * pairs,)),
             pltpu.SemaphoreType.DMA,
             pltpu.SemaphoreType.DMA((planes,)),
-            pltpu.SemaphoreType.REGULAR,
         ],
         compiler_params=pltpu.CompilerParams(
             has_side_effects=True, collective_id=0, vmem_limit_bytes=56 * 1024 * 1024

time: 79.6 us -> 78.3 us (0.984)
  Pallas kernels: 78.3 us -> 77 us
    pallas_call x1, Pallas kernels: 78.3 us -> 77 us  [helped_advance(): pl.pallas_call(step_kernel, in_specs=[pl.BlockSpec(memory_space=pl.ANY)]...]
where the time goes in v5:
time: 78.3 us; the launch traced here: 78.2 us
  Pallas kernels  77 us (98%)
  local copies, waits for them, and re-layouts  1.15 us (1%)
    pallas_call x1, Pallas kernels, helped_advance(): pl.pallas_call(step_kernel, in_specs=[pl.BlockSpec(memory_space=pl.ANY)]...  77 us

profile of v5, /device:TPU:3, one launch (start us, length us, event | category | flops | bytes accessed | tf_op | source)
XLA Modules:
  0.0 78.2 jit_solution(5657930190426248866)
XLA Ops:
  0.0 77.0 %step.1 = f32[3,128,8,128]{3,2,1,0:T(8,128)S(1)} custom-call(f32[3,128,8,128]{3,2,1,0:T(8,128)} %bitcast.5, f32[128,128]{1,0:T(8,128)} %constant.34.clone.refs_1_, bf16[4,96,256]{2,1,0:T(8,128)(2,1)} %constant.35.clone.refs_2_, bf16[4,96,256]{2,1,0:T(8,128)(2,1)} %constant.36.clone.refs_3_, bf16[128,256]{1,0:T(8,128)(2,1)} %constant.37.clone.refs_4_, ...), custom_call_target="tpu_custom_call" | custom-call | tf_op jit(solution)/shard_map/step/pallas_call | solution.py:882
  77.0 1.1 %copy.21 = f32[1,3,128,8,1,128]{5,4,3,2,1,0:T(1,128)} copy(f32[1,3,128,8,1,128]{5,4,3,2,1,0:T(1,128)S(1)} %bitcast.4) | data formatting | bytes 3145728

commit v6 on v5

--- a/solution.py
+++ b/solution.py
@@ -553,7 +553,7 @@
     crossing = 6
     late = 8
 
-    def transform(step, slot, high, half):
+    def transform(step, slot, high, half, kept=(1, 2, 0)):
         owner = pair_member if slot else member
         top_row = high * band + half * few
         fields = [rebuild(slot, top_row + a, owner) for a in range(few)]
@@ -563,7 +563,7 @@
         mean_slots = chunk * near_group
         complete = step % 2 == 1
         operands = []
-        for f in (1, 2, 0):
+        for f in kept:
             parts = [fields[a][f] for a in range(few)]
             stacked = jnp.concatenate(
                 [
@@ -574,9 +574,11 @@
             )
             operands.append((f, split(stacked)))
 
-        def deliver(target, place_in, away):
+        def deliver(target, place_in, away, only=kept):
             tables = (xi0[target * 2 + side], xi1[target * 2 + side])
             for f, stacked in operands:
+                if f not in only:
+                    continue
                 count = 2 if f else 1
                 moved = dot3([t[: count * points] for t in tables], stacked)
                 for p in range(planes):
@@ -596,59 +598,59 @@
                 if complete:
                     recv_mean[:, mean_slots + spot] = spread_mean[place_in // 2, :, spot]
 
-            def send(other, first, count, index, mean_index):
+            def send(other, k):
                 to = device(target, other // near, side * near + lax.rem(other, near))
-                remote(
-                    spread.at[place_in, pl.ds(2 * first, 2 * count), other],
-                    recv.at[pl.ds(2 * first, 2 * count), slots + spot],
-                    field_send,
-                    field_recv.at[index],
-                    to,
-                ).start()
+                if only != (0,):
+                    remote(
+                        spread.at[place_in, pl.ds(2 * k, 2), other],
+                        recv.at[pl.ds(2 * k, 2), slots + spot],
+                        field_send,
+                        field_recv.at[field_class(place_in) * pairs + k],
+                        to,
+                    ).start()
                 if complete:
                     remote(
-                        spread_mean.at[place_in // 2, pl.ds(first, count), other],
-                        recv_mean.at[pl.ds(first, count), mean_slots + spot],
+                        spread_mean.at[place_in // 2, k, other],
+                        recv_mean.at[k, mean_slots + spot],
                         field_send,
-                        mean_recv.at[mean_index],
+                        mean_recv.at[mean_class(place_in) * pairs + k],
                         to,
                     ).start()
 
-            index, mean_index = field_index(place_in), mean_index_of(place_in)
-            spans = [(0, pairs, index, mean_index)]
-            if step in (final, late + 1):
-                spans = [(k, 1, index + k, mean_index + k) for k in range(pairs)]
-            for span in spans:
-
-                def push(turn_index, carry, span=span, send=send):
-                    send(lax.rem(spot + near_group - turn_index, near_group), *span)
-                    return carry
-
-                lax.fori_loop(0 if away else 1, near_group, push, 0)
+            def emit(*parts):
+                for k in parts:
+
+                    def push(turn_index, carry, k=k):
+                        send(lax.rem(spot + near_group - turn_index, near_group), k)
+                        return carry
+
+                    lax.fori_loop(0 if away else 1, near_group, push, 0)
+
+            return emit
 
         if step in (final - 1, final):
 
             @pl.when(position == 0)
             def _():
-                deliver(1, step + 2, True)
-
-        deliver(position, step, False)
-
-    def field_index(place_in):
-        if place_in >= late:
-            place_in -= 2
-        return place_in if place_in <= final else place_in - 1 + pairs
-
-    def mean_index_of(place_in):
-        return place_in // 2 if place_in <= final else final // 2 + pairs
-
-    def await_fields(first, count, index, senders):
-        some = recv.at[pl.ds(2 * first, 2 * count), pl.ds(0, senders)]
-        remote(some, some, field_send, field_recv.at[index], beside).wait_recv()
-
-    def await_means(first, count, index, senders):
-        some = recv_mean.at[pl.ds(first, count), pl.ds(0, senders)]
-        remote(some, some, field_send, mean_recv.at[index], beside).wait_recv()
+                emit = deliver(1, step + 2, True, kept if step == final else (0,))
+                if complete:
+                    emit(*range(pairs))
+
+        return deliver(position, step, False)
+
+    def field_class(place_in):
+        return place_in if place_in <= final else place_in - 2 if place_in >= late else place_in
+
+    def mean_class(place_in):
+        return min(place_in // 2, final // 2 + 1)
+
+    def await_fields(k, kind, senders):
+        some = recv.at[pl.ds(2 * k, 2), pl.ds(0, senders)]
+        remote(some, some, field_send, field_recv.at[kind * pairs + k], beside).wait_recv()
+
+    def await_means(k, kind, senders):
+        some = recv_mean.at[k, pl.ds(0, senders)]
+        remote(some, some, field_send, mean_recv.at[kind * pairs + k], beside).wait_recv()
 
     low, high = list(range(band)), list(range(band, rows))
     own_order = high + low[::-1]
@@ -666,9 +668,9 @@
     def take_pair(rows_of):
         for a in rows_of:
             pair_copy(a).wait_recv()
-            if a in high:
-
-                @pl.when(position == 1)
+            if a in high or a < few:
+
+                @pl.when(position == (1 if a in high else 0))
                 def _():
                     relay_copy(a).start()
 
@@ -690,47 +692,75 @@
         if i not in needed:
             load.wait()
     on(1, lambda: take_own(high[:few]))
-    transform(0, 0, 1, 0)
+    rest, every = range(1, pairs), range(pairs)
+
+    def emit_all(*emits):
+        for k in every:
+            for emit in emits:
+                emit(k)
+
+    emit_0 = transform(0, 0, 1, 0)
+    on(0, lambda: emit_0(0))
+    on(1, lambda: emit_0(*every))
     on(0, lambda: send_pair(low[2:3]))
     on(1, lambda: take_own(high[few:]))
-    transform(1, 0, 1, 1)
+    emit_1 = transform(1, 0, 1, 1)
+    on(0, lambda: emit_1(0))
+    on(1, lambda: emit_1(*every))
     on(0, lambda: send_pair(low[3:]))
     on(1, lambda: take_own(low[few:][::-1]))
     on(1, lambda: take_pair(high[:1]))
-    transform(2, 0, 0, 1)
+    emit_2 = transform(2, 0, 0, 1)
+    on(0, lambda: emit_2(0))
+    on(1, lambda: emit_2(*every))
     on(1, lambda: take_own(low[:few][::-1]))
-    transform(3, 0, 0, 0)
+    emit_3 = transform(3, 0, 0, 0)
+    emit_3(0)
+
+    def emit_own():
+        for k in rest:
+            for emit in (emit_0, emit_1, emit_2, emit_3):
+                emit(k)
+
+    on(0, emit_own)
     on(0, lambda: take_pair(low[:few]))
     on(1, lambda: take_pair(high[1:few]))
-    transform(4, 1, position, 0)
+    emit_4 = transform(4, 1, position, 0)
+    emit_4(0)
+    on(1, lambda: emit_3(*rest))
+    emit_4(*rest)
     on(0, lambda: take_pair(low[few:]))
     on(1, lambda: take_pair(high[few:]))
-    transform(5, 1, position, 1)
+    emit_5 = transform(5, 1, position, 1)
 
     def finish_late():
+        emit_5(0)
         take_pair(high[:few])
-        transform(late, 1, 1, 0)
+        emit_6 = transform(late, 1, 1, 0)
+        emit_6(0)
+        emit_5(*rest)
+        emit_6(*rest)
         take_pair(high[few:])
-        transform(late + 1, 1, 1, 1)
+        transform(late + 1, 1, 1, 1)(*every)
+
+    def join_late():
+        take_pair(low[:few])
+        emit_all(emit_5, transform(late, 1, 0, 0, (1, 2)))
 
     on(0, finish_late)
-
-    for step in range(final):
-        await_fields(0, pairs, step, near_group - 1)
-    for step in range(final // 2):
-        await_means(0, pairs, step, near_group - 1)
-    on(0, lambda: await_fields(0, pairs, field_index(crossing), near_group - 1))
-    on(1, lambda: await_fields(0, pairs, field_index(crossing), near_group))
+    on(1, join_late)
 
     tables = [ref[...] for ref in plane_refs]
 
     def plane_pair(k, carry):
-        await_fields(k, 1, final + k, near_group - 1)
-        await_means(k, 1, final // 2 + k, near_group - 1)
+        for kind in range(7):
+            await_fields(k, kind, near_group - 1)
+        for kind in range(3):
+            await_means(k, kind, near_group - 1)
 
         def await_last(senders):
-            await_fields(k, 1, field_index(crossing + 1) + k, senders)
-            await_means(k, 1, mean_index_of(crossing) + k, senders)
+            await_fields(k, 7, senders)
+            await_means(k, 3, senders)
 
         on(0, lambda: await_last(near_group - 1))
         on(1, lambda: await_last(near_group))
@@ -848,18 +878,24 @@
     @pl.when(position == 0)
     def _():
         await_sends(
-            spread.at[pl.ds(crossing, 2)],
+            spread.at[crossing + 1],
             spread_mean.at[crossing // 2],
             spread.at[pl.ds(late, 2), :, others],
             spread_mean.at[late // 2, :, others],
         )
 
+    @pl.when(position == 1)
+    def _():
+        await_sends(spread.at[late, :, others])
+
     some = modes.at[1, pl.ds(0, band)]
     remote(modes.at[0], modes.at[0], mode_send, own_recv.at[0], beside).wait_send()
 
     @pl.when(position == 0)
     def _():
         remote(some, some, mode_send, own_recv.at[0], beside).wait_send()
+        relayed = modes.at[1, pl.ds(0, few)]
+        remote(relayed, relayed, mode_send, own_recv.at[0], beside).wait_send()
         remote(result, result, back_send, back_recv.at[0], beside).wait_send()
 
     @pl.when(position == 1)
@@ -902,8 +938,8 @@
             pltpu.SemaphoreType.DMA((rows,)),
             pltpu.SemaphoreType.DMA((rows,)),
             pltpu.SemaphoreType.DMA,
-            pltpu.SemaphoreType.DMA((6 + 2 * pairs,)),
-            pltpu.SemaphoreType.DMA((2 + 2 * pairs,)),
+            pltpu.SemaphoreType.DMA((8 * pairs,)),
+            pltpu.SemaphoreType.DMA((4 * pairs,)),
             pltpu.SemaphoreType.DMA,
             pltpu.SemaphoreType.DMA((planes,)),
         ],

time: 78.3 us -> 77.9 us (level)
  no operation moved by 1% of the time
where the time goes in v6:
time: 77.9 us; the launch traced here: 77.8 us
  Pallas kernels  76.6 us (98%)
  local copies, waits for them, and re-layouts  1.15 us (1%)
    pallas_call x1, Pallas kernels, helped_advance(): pl.pallas_call(step_kernel, in_specs=[pl.BlockSpec(memory_space=pl.ANY)]...  76.6 us

profile of v6, /device:TPU:3, one launch (start us, length us, event | category | flops | bytes accessed | tf_op | source)
XLA Modules:
  0.0 77.8 jit_solution(18297405908072230023)
XLA Ops:
  0.0 76.6 %step.1 = f32[3,128,8,128]{3,2,1,0:T(8,128)S(1)} custom-call(f32[3,128,8,128]{3,2,1,0:T(8,128)} %bitcast.5, f32[128,128]{1,0:T(8,128)} %constant.34.clone.refs_1_, bf16[4,96,256]{2,1,0:T(8,128)(2,1)} %constant.35.clone.refs_2_, bf16[4,96,256]{2,1,0:T(8,128)(2,1)} %constant.36.clone.refs_3_, bf16[128,256]{1,0:T(8,128)(2,1)} %constant.37.clone.refs_4_, ...), custom_call_target="tpu_custom_call" | custom-call | tf_op jit(solution)/shard_map/step/pallas_call | solution.py:918
  76.6 1.1 %copy.21 = f32[1,3,128,8,1,128]{5,4,3,2,1,0:T(1,128)} copy(f32[1,3,128,8,1,128]{5,4,3,2,1,0:T(1,128)S(1)} %bitcast.4) | data formatting | bytes 3145728

commit v7 on v6

--- a/solution.py
+++ b/solution.py
@@ -460,6 +460,9 @@
         pltpu.make_async_copy(source, target, table_sem.at[i])
         for i, (source, target) in enumerate(zip(kept_tables, loaded))
     ]
+    modes[:, 1:, 2 * retained : 2 * retained + 8, :] = jnp.zeros(
+        (2, rows - 1, 8, retained), jnp.float32
+    )
     needed = (0, 7)
     for i in needed:
         loads[i].start()
@@ -508,7 +511,11 @@
             turning = (wave_y * values[2] - wave_z * values[1]) * inverse
             modes[0, a, 0:retained, :] = jnp.where(still, values[1], values[0])
             modes[0, a, retained : 2 * retained, :] = jnp.where(still, values[2], turning)
-            modes[0, a, 2 * retained : 2 * retained + 8, :] = values[0][0:8]
+
+            @pl.when(a == 0)
+            def _():
+                modes[0, 0, 2 * retained : 2 * retained + 8, :] = values[0][0:8]
+
             return carry
 
         lax.fori_loop(start, stop, first, 0)
@@ -532,14 +539,17 @@
         v2 = jnp.where(still, second, -(wave_z * inverse) * pushed + wave_y * second)
         return v0, v1, v2
 
+    def sent_rows(slot, a):
+        return modes.at[slot, a, pl.ds(0, 2 * retained + (0 if a else 8))]
+
     def own_copy(a):
-        return remote(modes.at[0, a], modes.at[0, a], mode_send, own_recv.at[a], across)
+        return remote(sent_rows(0, a), sent_rows(0, a), mode_send, own_recv.at[a], across)
 
     def pair_copy(a):
-        return remote(modes.at[0, a], modes.at[1, a], mode_send, pair_recv.at[a], beside)
+        return remote(sent_rows(0, a), sent_rows(1, a), mode_send, pair_recv.at[a], beside)
 
     def relay_copy(a):
-        return remote(modes.at[1, a], modes.at[1, a], mode_send, pair_recv.at[a], across)
+        return remote(sent_rows(1, a), sent_rows(1, a), mode_send, pair_recv.at[a], across)
 
     def each(start, stop, do):
         def body(a, carry):
@@ -888,18 +898,21 @@
     def _():
         await_sends(spread.at[late, :, others])
 
-    some = modes.at[1, pl.ds(0, band)]
-    remote(modes.at[0], modes.at[0], mode_send, own_recv.at[0], beside).wait_send()
-
     @pl.when(position == 0)
     def _():
-        remote(some, some, mode_send, own_recv.at[0], beside).wait_send()
-        relayed = modes.at[1, pl.ds(0, few)]
-        remote(relayed, relayed, mode_send, own_recv.at[0], beside).wait_send()
+        for a in low + high:
+            own_copy(a).wait_send()
+        for a in low:
+            pair_copy(a).wait_send()
+        for a in low[:few]:
+            relay_copy(a).wait_send()
         remote(result, result, back_send, back_recv.at[0], beside).wait_send()
 
     @pl.when(position == 1)
     def _():
+        for a in high:
+            pair_copy(a).wait_send()
+            relay_copy(a).wait_send()
         some = result.at[:, pl.ds(0, groups - 1)]
         remote(some, some, back_send, back_recv.at[0], beside).wait_send()
 

time: 77.9 us -> 77.1 us (0.990)
  Pallas kernels: 76.6 us -> 75.8 us
    pallas_call x1, Pallas kernels: 76.6 us -> 75.8 us  [helped_advance(): pl.pallas_call(step_kernel, in_specs=[pl.BlockSpec(memory_space=pl.ANY)]...]
where the time goes in v7:
time: 77.1 us; the launch traced here: 76.9 us
  Pallas kernels  75.8 us (98%)
  local copies, waits for them, and re-layouts  1.15 us (1%)
    pallas_call x1, Pallas kernels, helped_advance(): pl.pallas_call(step_kernel, in_specs=[pl.BlockSpec(memory_space=pl.ANY)]...  75.8 us

profile of v7, /device:TPU:3, one launch (start us, length us, event | category | flops | bytes accessed | tf_op | source)
XLA Modules:
  0.0 76.9 jit_solution(11654489605220421607)
XLA Ops:
  0.0 75.8 %step.1 = f32[3,128,8,128]{3,2,1,0:T(8,128)S(1)} custom-call(f32[3,128,8,128]{3,2,1,0:T(8,128)} %bitcast.5, f32[128,128]{1,0:T(8,128)} %constant.34.clone.refs_1_, bf16[4,96,256]{2,1,0:T(8,128)(2,1)} %constant.35.clone.refs_2_, bf16[4,96,256]{2,1,0:T(8,128)(2,1)} %constant.36.clone.refs_3_, bf16[128,256]{1,0:T(8,128)(2,1)} %constant.37.clone.refs_4_, ...), custom_call_target="tpu_custom_call" | custom-call | tf_op jit(solution)/shard_map/step/pallas_call | solution.py:931
  75.8 1.1 %copy.21 = f32[1,3,128,8,1,128]{5,4,3,2,1,0:T(1,128)} copy(f32[1,3,128,8,1,128]{5,4,3,2,1,0:T(1,128)S(1)} %bitcast.4) | data formatting | bytes 3145728

commit v8 on v7

--- a/solution.py
+++ b/solution.py
@@ -710,35 +710,23 @@
                 emit(k)
 
     emit_0 = transform(0, 0, 1, 0)
-    on(0, lambda: emit_0(0))
-    on(1, lambda: emit_0(*every))
+    emit_0(*every)
     on(0, lambda: send_pair(low[2:3]))
     on(1, lambda: take_own(high[few:]))
     emit_1 = transform(1, 0, 1, 1)
-    on(0, lambda: emit_1(0))
-    on(1, lambda: emit_1(*every))
+    emit_1(*every)
     on(0, lambda: send_pair(low[3:]))
     on(1, lambda: take_own(low[few:][::-1]))
     on(1, lambda: take_pair(high[:1]))
     emit_2 = transform(2, 0, 0, 1)
-    on(0, lambda: emit_2(0))
-    on(1, lambda: emit_2(*every))
+    emit_2(*every)
     on(1, lambda: take_own(low[:few][::-1]))
     emit_3 = transform(3, 0, 0, 0)
-    emit_3(0)
-
-    def emit_own():
-        for k in rest:
-            for emit in (emit_0, emit_1, emit_2, emit_3):
-                emit(k)
-
-    on(0, emit_own)
+    emit_3(*every)
     on(0, lambda: take_pair(low[:few]))
     on(1, lambda: take_pair(high[1:few]))
     emit_4 = transform(4, 1, position, 0)
-    emit_4(0)
-    on(1, lambda: emit_3(*rest))
-    emit_4(*rest)
+    emit_4(*every)
     on(0, lambda: take_pair(low[few:]))
     on(1, lambda: take_pair(high[few:]))
     emit_5 = transform(5, 1, position, 1)
@@ -793,7 +781,7 @@
 
             def push(turn_index, carry):
                 to_place = lax.rem(place + near + turn_index // count_py, count_pz)
-                to_row = lax.rem(row + turn_index, count_py)
+                to_row = lax.rem(row + turn_index + p, count_py)
                 to_member = to_row * count_pz + to_place
 
                 @pl.when(jnp.logical_or(position == 0, to_member != member))

time: 77.1 us -> 77.2 us (level)
  no operation moved by 1% of the time
where the time goes in v8:
time: 77.2 us; the launch traced here: 77 us
  Pallas kernels  75.9 us (98%)
  local copies, waits for them, and re-layouts  1.15 us (1%)
    pallas_call x1, Pallas kernels, helped_advance(): pl.pallas_call(step_kernel, in_specs=[pl.BlockSpec(memory_space=pl.ANY)]...  75.9 us

profile of v8, /device:TPU:3, one launch (start us, length us, event | category | flops | bytes accessed | tf_op | source)
XLA Modules:
  0.0 77.0 jit_solution(12658440402432219868)
XLA Ops:
  0.0 75.9 %step.1 = f32[3,128,8,128]{3,2,1,0:T(8,128)S(1)} custom-call(f32[3,128,8,128]{3,2,1,0:T(8,128)} %bitcast.5, f32[128,128]{1,0:T(8,128)} %constant.34.clone.refs_1_, bf16[4,96,256]{2,1,0:T(8,128)(2,1)} %constant.35.clone.refs_2_, bf16[4,96,256]{2,1,0:T(8,128)(2,1)} %constant.36.clone.refs_3_, bf16[128,256]{1,0:T(8,128)(2,1)} %constant.37.clone.refs_4_, ...), custom_call_target="tpu_custom_call" | custom-call | tf_op jit(solution)/shard_map/step/pallas_call | solution.py:919
  75.9 1.1 %copy.21 = f32[1,3,128,8,1,128]{5,4,3,2,1,0:T(1,128)} copy(f32[1,3,128,8,1,128]{5,4,3,2,1,0:T(1,128)S(1)} %bitcast.4) | data formatting | bytes 3145728
